TPU v7x, 32 devices: a whole 2x2x4 slice. The times are simulated.
32 devices in a mesh: pp: 4 (over z), dp: 8 (over y, x, core).
Axes of the slice: x: 2, y: 2, z: 4, core: 2. Of those that a mesh axis runs over, the one named last changes fastest.
Arguments:
- tok_ids: int32 [4, 256], P(None, 'dp')
- d_out: bfloat16 [4, 256, 512], P('pp', 'dp')
- stored_x: bfloat16 [4, 4, 256, 512], P('pp', None, 'dp')
- w_in: bfloat16 [12, 512, 2048], P('pp')
- w_out: bfloat16 [12, 2048, 512], P('pp')
- acc_in: float32 [12, 8, 512, 2048], P('pp', 'dp')
- acc_out: float32 [12, 8, 2048, 512], P('pp', 'dp')
- acc_emb: float32 [8, 30522, 512], P('dp')
Outputs:
- output 1: float32 [12, 512, 2048], P('pp', 'dp')
- output 2: float32 [12, 2048, 512], P('pp', 'dp')
- output 3: float32 [30522, 512], P(None, 'dp')
All inputs are finite; a program needn't handle non-finite values.
Results may differ from a plain program's by a relative error of at most 0.01615.
Values are sent between devices in bfloat16 or wider.
A program may use at most 1 GiB of HBM per device.

v0:
```python
import jax
import jax.numpy as jnp
from jax import lax
from jax.sharding import PartitionSpec as P


def layer_forward(x_cur, w_in_l, w_out_l):
    pre_act = jnp.dot(x_cur, w_in_l, preferred_element_type=jnp.float32).astype(jnp.bfloat16)
    hidden = jax.nn.gelu(pre_act.astype(jnp.float32)).astype(jnp.bfloat16)
    out_x = (x_cur.astype(jnp.float32) + jnp.dot(hidden, w_out_l, preferred_element_type=jnp.float32)).astype(jnp.bfloat16)
    return out_x, pre_act, hidden


def layer_backward(cot_cur, w_in_l, w_out_l, x_cur, pre_act, hidden):
    g_out = jnp.einsum('tf,th->fh', hidden, cot_cur, preferred_element_type=jnp.float32)
    d_hidden = jnp.einsum('th,fh->tf', cot_cur, w_out_l, preferred_element_type=jnp.float32).astype(jnp.bfloat16)
    pre_f = pre_act.astype(jnp.float32)
    gelu_slope = jax.jvp(jax.nn.gelu, (pre_f,), (jnp.ones_like(pre_f),))[1]
    d_pre = (d_hidden.astype(jnp.float32) * gelu_slope).astype(jnp.bfloat16)
    g_in = jnp.einsum('th,tf->hf', x_cur, d_pre, preferred_element_type=jnp.float32)
    d_x = (cot_cur.astype(jnp.float32) + jnp.einsum('tf,hf->th', d_pre, w_in_l, preferred_element_type=jnp.float32)).astype(jnp.bfloat16)
    return d_x, g_in, g_out


def cooldown_local(tok_ids, d_out, stored_x, w_in, w_out, acc_in, acc_out, acc_emb, stages):
    stage_id = lax.axis_index('pp')
    layers = w_in.shape[0]
    hid_size = d_out.shape[2]
    sums_in = [acc_in[layer_id, 0] for layer_id in range(layers)]
    sums_out = [acc_out[layer_id, 0] for layer_id in range(layers)]
    is_first = stage_id == 0
    cot_recv = d_out[0]
    first_dx = []
    for step_id in range(stages):
        left_over = stages - 1 - stage_id - step_id
        active = left_over >= 0
        micro_id = jnp.maximum(left_over, 0)
        x_cur = lax.dynamic_index_in_dim(stored_x[0], micro_id, axis=0, keepdims=False)
        saved_acts = []
        for layer_id in range(layers):
            out_x, pre_act, hidden = layer_forward(x_cur, w_in[layer_id], w_out[layer_id])
            saved_acts.append((x_cur, pre_act, hidden))
            x_cur = out_x
        cot_cur = cot_recv
        for layer_id in range(layers - 1, -1, -1):
            x_in, pre_act, hidden = saved_acts[layer_id]
            cot_cur, g_in, g_out = layer_backward(cot_cur, w_in[layer_id], w_out[layer_id], x_in, pre_act, hidden)
            sums_in[layer_id] = sums_in[layer_id] + jnp.where(active, g_in, 0.0)
            sums_out[layer_id] = sums_out[layer_id] + jnp.where(active, g_out, 0.0)
        first_dx.append(cot_cur)
        if step_id < stages - 1:
            cot_recv = lax.ppermute(cot_cur, 'pp', [(sender, sender - 1) for sender in range(1, stages)])
    dx_all = jnp.stack(first_dx).reshape(-1, hid_size).astype(jnp.float32)
    ids_steps = tok_ids[::-1].reshape(-1)
    emb_sum = acc_emb[0].at[ids_steps].add(jnp.where(is_first, dx_all, 0.0))
    return jnp.stack(sums_in), jnp.stack(sums_out), emb_sum, is_first


def replica_average(local_sum, replicas):
    summed = lax.psum_scatter(local_sum.astype(jnp.bfloat16), 'dp', scatter_dimension=1, tiled=True)
    return summed.astype(jnp.float32) / replicas


def solution(mesh):
    stages = mesh.shape['pp']
    replicas = mesh.shape['dp']

    def device_body(tok_ids, d_out, stored_x, w_in, w_out, acc_in, acc_out, acc_emb):
        sum_in, sum_out, emb_sum, is_first = cooldown_local(tok_ids, d_out, stored_x, w_in, w_out, acc_in, acc_out, acc_emb, stages)
        grad_in = replica_average(sum_in, replicas)
        grad_out = replica_average(sum_out, replicas)
        vocab_rows = emb_sum.shape[0]
        piece_cols = emb_sum.shape[1] // (replicas * stages)
        emb_split = jnp.where(is_first, emb_sum, 0.0).astype(jnp.bfloat16).reshape(vocab_rows, replicas, stages, piece_cols)
        own_piece = emb_split[:, :, 0, :]
        for target in range(1, stages):
            own_piece = own_piece + lax.ppermute(emb_split[:, :, target, :], 'pp', [(0, target)])
        summed = lax.psum_scatter(own_piece, 'dp', scatter_dimension=1, tiled=True)
        gathered = lax.all_gather(summed[:, 0, :], 'pp', axis=1)
        grad_emb = gathered.reshape(vocab_rows, stages * piece_cols).astype(jnp.float32) / replicas
        return grad_in, grad_out, grad_emb

    return jax.shard_map(device_body, mesh=mesh, in_specs=(P(None, 'dp'), P('pp', 'dp', None), P('pp', None, 'dp', None), P('pp', None, None), P('pp', None, None), P('pp', 'dp', None, None), P('pp', 'dp', None, None), P('dp', None, None)), out_specs=(P('pp', 'dp', None), P('pp', 'dp', None), P(None, 'dp')), check_vma=False)
```

profile of v0, /device:TPU:25, one launch (start us, length us, event | category | flops | bytes accessed | tf_op | source)
XLA Modules:
  0.0 1025.3 jit_solution(11211519921334295331)
XLA Ops:
  7.2 2.1 fusion.77
  9.3 2.2 fusion.218
  11.5 2.4 fusion.76
  17.1 2.5 fusion.80
  24.0 2.1 collective-permute-start
  26.1 2.1 fusion.65
  28.2 2.2 fusion.215
  30.4 2.2 fusion.64
  32.6 2.1 fusion.200
  47.5 2.8 collective-permute-start.1
  51.7 2.3 fusion.56
  54.0 2.4 add_convert_fusion.3
  56.5 2.3 fusion.50
  58.8 2.4 add_convert_fusion.2
  61.2 2.3 fusion.47
  63.5 2.4 fusion.224
  65.9 2.6 collective-permute-start.2
  68.5 41.7 %copy.33 = f32[1,30522,512]{2,1,0:T(8,128)} copy(f32[1,30522,512]{2,0,1:T(1,128)} %param.15) | data formatting | bytes 125018112
  110.2 2.3 fusion.44
  112.6 2.4 add_convert_fusion.1
  115.0 2.3 fusion.38
  117.3 2.4 add_convert_fusion
  119.7 2.3 fusion.35
  122.1 2.4 fusion.233
  125.3 15.9 %scatter_fusion = f32[30522,512]{1,0:T(8,128)} fusion(f32[30522,512]{1,0:T(8,128)} %bitcast.373, s32[128]{0:T(128)S(1)} %fusion.444, f32[128,512]{1,0:T(8,128)S(1)} %bitcast.379), kind=kCustom, calls=%fused_computation | custom fusion | flops 65536 | bytes 786944 | tf_op jit(solution)/shard_map/scatter-add | solution.py:55
  141.2 11.1 %select_convert_fusion = bf16[30522,512]{1,0:T(8,128)(2,1)} fusion(f32[30522,512]{1,0:T(8,128)} %scatter_fusion, pred[]{:T(512)S(6)} %eq.3), kind=kLoop, calls=%fused_computation.2 | loop fusion | flops 15627264 | bytes 93763584 | tf_op jit(solution)/shard_map/convert_element_type | solution.py:74
  152.3 40.8 %copy.24 = bf16[30522,512]{0,1:T(8,128)(2,1)} copy(bf16[30522,512]{1,0:T(8,128)(2,1)} %select_convert_fusion) | data formatting | bytes 62509056 | tf_op jit(solution)/shard_map/convert_element_type | solution.py:74
  193.1 11.3 %slice_bitcast_fusion.2 = (bf16[30522,8,16]{0,2,1:T(8,128)(2,1)}, bf16[30522,8,16]{0,2,1:T(8,128)(2,1)S(1)}, bf16[30522,8,16]{0,2,1:T(8,128)(2,1)S(1)}) fusion(bf16[30522,8,4,16]{0,3,2,1:T(8,128)(2,1)} %bitcast.374), kind=kLoop, calls=%fused_computation.5 | loop fusion | bytes 46881792 | tf_op jit(solution)/shard_map/squeeze | solution.py:77
  206.8 3.7 collective-permute-start.4
  210.6 349.4 %collective-permute-done.5 = bf16[30522,8,16]{0,2,1:T(8,128)(2,1)S(1)} collective-permute-done((bf16[30522,8,16]{0,2,1:T(8,128)(2,1)S(1)}, bf16[30522,8,16]{0,2,1:T(8,128)(2,1)S(1)}, u32[]{:S(2)}, u32[]{:S(2)}) %collective-permute-start.5) | collective-permute-done | bytes 7813664 | tf_op jit(solution)/shard_map/ppermute | solution.py:77
  559.9 8.8 fusion.2
  574.4 2.8 fusion.465
  579.5 5.5 fusion.30
  585.0 4.1 fusion.31
  589.1 4.2 fusion.32
  593.3 3.1 pad_maximum_fusion.1
  602.0 2.8 fusion.417
  606.2 5.5 fusion.27
  611.7 4.0 fusion.28
  615.7 4.0 fusion.29
  619.8 3.2 pad_maximum_fusion
  623.0 185.6 %reduce-scatter.8.cloned.1.call-done = bf16[30522,1,16]{0,2,1:T(8,128)(2,1)} async-done(((bf16[30522,8,16]{0,2,1:T(8,128)(2,1)}), bf16[30522,1,16]{0,2,1:T(8,128)(2,1)}) %reduce-scatter.8.cloned.1.call-update) | async-done | bytes 976720 | tf_op jit(solution)/shard_map/reduce_scatter | solution.py:78
  808.6 64.5 %reduce-scatter.6.cloned.1.call-done = bf16[3,256,512]{2,1,0:T(8,128)(2,1)} async-done(((bf16[3,2048,512]{2,1,0:T(8,128)(2,1)}), bf16[3,256,512]{2,1,0:T(8,128)(2,1)}) %reduce-scatter.6.cloned.1.call-update) | async-done | bytes 786448 | tf_op jit(solution)/shard_map/reduce_scatter | solution.py:60
  873.1 2.5 convert_multiply_fusion.1
  875.6 62.1 %reduce-scatter.4.cloned.1.call-done = bf16[3,64,2048]{2,1,0:T(8,128)(2,1)} async-done(((bf16[3,512,2048]{2,1,0:T(8,128)(2,1)}), bf16[3,64,2048]{2,1,0:T(8,128)(2,1)}) %reduce-scatter.4.cloned.1.call-update) | async-done | bytes 786448 | tf_op jit(solution)/shard_map/reduce_scatter | solution.py:60
  937.7 2.5 convert_multiply_fusion.2
  940.1 72.4 %all-gather.2.cloned.1.call-done = bf16[30522,4,16]{0,2,1:T(8,128)(2,1)} async-done(((bf16[30522,1,16]{0,2,1:T(8,128)(2,1)}), bf16[30522,4,16]{0,2,1:T(8,128)(2,1)}) %all-gather.2.cloned.1.call-update) | async-done | bytes 3906832 | tf_op jit(solution)/shard_map/all_gather | solution.py:79
  1012.5 5.8 convert_multiply_fusion
  (217 shorter events, 39.4 us)
Async XLA Ops:
  7.2 801.5 %reduce-scatter.8.cloned.1.call-start = ((), (), s32[]{:S(2)}) async-start(), calls=%async_computation.5 | async-start | bytes 8810496 | tf_op jit(solution)/shard_map/reduce_scatter | solution.py:78
  9.3 12.6 %copy-start.14 = (f32[32,2048]{1,0:T(8,128)}, f32[32,2048]{1,0:T(8,128)S(1)}, u32[]{:S(2)}) copy-start(f32[32,2048]{1,0:T(8,128)S(1)} %fusion.77) | copy-start | bytes 786436
  9.3 7.3 copy-start
  11.5 5.5 copy-start.59
  16.6 3.8 copy-start.73
  21.1 7.0 copy-start.43
  21.1 5.0 copy-start.20
  22.6 10.0 copy-start.45
  22.6 12.1 %slice-start = ((s8[6291456]{0:T(1024)(128)(4,1)}), s8[2097152]{0:T(1024)(128)(4,1)S(1)}, s32[]{:S(2)}) async-start(s8[6291456]{0:T(1024)(128)(4,1)} %bitcast.376), calls=%async_computation.7 | async-start | bytes 4194304
  24.0 18.4 %collective-permute-start = (bf16[32,512]{1,0:T(8,128)(2,1)}, bf16[32,512]{1,0:T(8,128)(2,1)S(1)}, u32[]{:S(2)}, u32[]{:S(2)}) collective-permute-start(bf16[32,512]{1,0:T(8,128)(2,1)} %fusion.230), channel_id=1, source_target_pairs={{8,0},{16,8},{24,16},{9,1},{17,9},{25,17},{10,2},{18,10},{26,18},{... | collective-permute-start | bytes 98312 | tf_op jit(solution)/shard_map/ppermute | solution.py:52
  28.1 17.3 %copy-start.18 = (f32[32,2048]{1,0:T(8,128)}, f32[32,2048]{1,0:T(8,128)S(1)}, u32[]{:S(2)}) copy-start(f32[32,2048]{1,0:T(8,128)S(1)} %fusion.65) | copy-start | bytes 786436
  28.1 6.6 slice-start.1
  30.4 4.4 copy-start.39
  30.4 8.1 slice-start.2
  32.6 11.3 %copy-start.9 = (f32[32,2048]{1,0:T(8,128)}, f32[32,2048]{1,0:T(8,128)S(1)}, u32[]{:S(2)}) copy-start(f32[32,2048]{1,0:T(8,128)S(1)} %fusion.64) | copy-start | bytes 786436
  34.8 7.2 copy-start.37
  34.8 3.7 slice-start.3
  39.0 11.4 %copy-start.33 = (bf16[32,512]{1,0:T(8,128)(2,1)}, bf16[32,512]{1,0:T(8,128)(2,1)S(1)}, u32[]{:S(2)}) copy-start(bf16[32,512]{1,0:T(8,128)(2,1)S(1)} %fusion.197) | copy-start | bytes 98308
  39.4 80.3 %copy-start.6 = (f32[32,2048]{1,0:T(8,128)}, f32[32,2048]{1,0:T(8,128)S(1)}, u32[]{:S(2)}) copy-start(f32[32,2048]{1,0:T(8,128)S(1)} %fusion.41) | copy-start | bytes 786436
  40.4 74.6 %copy-start.5 = (f32[32,2048]{1,0:T(8,128)}, f32[32,2048]{1,0:T(8,128)S(1)}, u32[]{:S(2)}) copy-start(f32[32,2048]{1,0:T(8,128)S(1)} %fusion.40) | copy-start | bytes 786436
  41.9 68.3 %copy-start.3 = (f32[32,2048]{1,0:T(8,128)}, f32[32,2048]{1,0:T(8,128)S(1)}, u32[]{:S(2)}) copy-start(f32[32,2048]{1,0:T(8,128)S(1)} %fusion.39) | copy-start | bytes 786436
  45.4 5.0 copy-start.64
  45.4 6.2 copy-start.72
  46.2 4.2 copy-start.53
  47.5 4.2 collective-permute-start.1
  54.0 9.5 copy-start.51
  54.0 7.2 copy-start.17
  58.8 51.4 %copy-start.55 = (bf16[32,2048]{1,0:T(8,128)(2,1)}, bf16[32,2048]{1,0:T(8,128)(2,1)S(1)}, u32[]{:S(2)}) copy-start(bf16[32,2048]{1,0:T(8,128)(2,1)S(1)} %fusion.50) | copy-start | bytes 393220
  63.5 46.7 %copy-start.57 = (bf16[32,2048]{1,0:T(8,128)(2,1)}, bf16[32,2048]{1,0:T(8,128)(2,1)S(1)}, u32[]{:S(2)}) copy-start(bf16[32,2048]{1,0:T(8,128)(2,1)S(1)} %fusion.47) | copy-start | bytes 393220
  65.9 44.3 %collective-permute-start.2 = (bf16[32,512]{1,0:T(8,128)(2,1)S(1)}, bf16[32,512]{1,0:T(8,128)(2,1)S(1)}, u32[]{:S(2)}, u32[]{:S(2)}) collective-permute-start(bf16[32,512]{1,0:T(8,128)(2,1)S(1)} %fusion.224), channel_id=1, source_target_pairs={{8,0},{16,8},{24,16},{9,1},{17,9},{25,17},{10,2},{18,10},{26,18},{... | collective-permute-start | bytes 98312 | tf_op jit(solution)/shard_map/ppermute | solution.py:52
  110.2 7.1 copy-start.60
  112.6 9.5 copy-start.22
  117.3 8.0 copy-start.24
  119.7 21.4 %copy-start.70 = (bf16[32,512]{1,0:T(8,128)(2,1)}, bf16[32,512]{1,0:T(8,128)(2,1)S(1)}, u32[]{:S(2)}) copy-start(bf16[32,512]{1,0:T(8,128)(2,1)S(1)} %add_convert_fusion) | copy-start | bytes 98308
  122.1 30.2 %copy-start.25 = (bf16[32,2048]{1,0:T(8,128)(2,1)}, bf16[32,2048]{1,0:T(8,128)(2,1)S(1)}, u32[]{:S(2)}) copy-start(bf16[32,2048]{1,0:T(8,128)(2,1)S(1)} %fusion.35) | copy-start | bytes 393220
  204.4 6.2 collective-permute-start.3
  205.5 354.4 %collective-permute-start.5 = (bf16[30522,8,16]{0,2,1:T(8,128)(2,1)S(1)}, bf16[30522,8,16]{0,2,1:T(8,128)(2,1)S(1)}, u32[]{:S(2)}, u32[]{:S(2)}) collective-permute-start(bf16[30522,8,16]{0,2,1:T(8,128)(2,1)S(1)} %get-tuple-element.4), channel_id=1, source_target_pairs={{0,24},{1,25},{2,26},{3,27},{4,28},{5,29},{6,30},{7,31}} | collective-permute-start | bytes 23440904 | tf_op jit(solution)/shard_map/ppermute | solution.py:77
  206.8 353.1 %collective-permute-start.4 = (bf16[30522,8,16]{0,2,1:T(8,128)(2,1)S(1)}, bf16[30522,8,16]{0,2,1:T(8,128)(2,1)}, u32[]{:S(2)}, u32[]{:S(2)}) collective-permute-start(bf16[30522,8,16]{0,2,1:T(8,128)(2,1)S(1)} %get-tuple-element.5), channel_id=1, source_target_pairs={{0,16},{1,17},{2,18},{3,19},{4,20},{5,21},{6,22},{7,23}} | collective-permute-start | bytes 23440904 | tf_op jit(solution)/shard_map/ppermute | solution.py:77
  568.8 304.3 %reduce-scatter.6.cloned.1.call-start = ((), (), s32[]{:S(2)}) async-start(), calls=%async_computation.4 | async-start | bytes 7077888 | tf_op jit(solution)/shard_map/reduce_scatter | solution.py:60
  579.4 5.5 copy-start.69
  585.0 4.2 copy-start.4
  585.0 4.2 copy-start.61
  589.1 4.2 copy-start.2
  596.5 341.2 %reduce-scatter.4.cloned.1.call-start = ((), (), s32[]{:S(2)}) async-start(), calls=%async_computation.3 | async-start | bytes 7077888 | tf_op jit(solution)/shard_map/reduce_scatter | solution.py:60
  611.7 4.0 copy-start.23
  611.7 4.0 copy-start.27
  615.7 4.0 copy-start.1
  623.0 389.5 %all-gather.2.cloned.1.call-start = ((), (), s32[]{:S(2)}) async-start(), calls=%async_computation.6 | async-start | bytes 4894720 | tf_op jit(solution)/shard_map/all_gather | solution.py:79
  (40 other events, 82.3 us)
Sparse Core Ops, SparseCore 0:
  568.9 239.6 reduce-scatter.7
  812.0 61.0 reduce-scatter.5
  876.5 61.1 reduce-scatter.3
  939.1 73.3 all-gather.1
where the time goes:
time: 1040 us; the launch traced here: 1030 us
  waiting for transfers between devices  734 us (71%)
  matrix products  111 us (11%)
  local copies, waits for them, and re-layouts  97.5 us (9%)
  other arithmetic  53.7 us (5%)
  between operations  15.4 us (1%)
  starting transfers between devices  14.3 us (1%)
    ppermute x3, waiting for transfers between devices, device_body(): lax.ppermute(emb_split[:, :, target, :], 'pp', [(0, target)])  349 us
    reduce_scatter x1, waiting for transfers between devices, device_body(): summed = lax.psum_scatter(own_piece, 'dp', scatter_dimension=1, tiled=True)  186 us
    reduce_scatter x2, waiting for transfers between devices, replica_average(): lax.psum_scatter(local_sum.astype(jnp.bfloat16), 'dp', scatter_dimension=...  127 us
    all_gather x1, waiting for transfers between devices, device_body(): gathered = lax.all_gather(summed[:, 0, :], 'pp', axis=1)  72.4 us
    unnamed x157, local copies, waits for them, and re-layouts  45.3 us
    convert_element_type x1, local copies, waits for them, and re-layouts, device_body(): jnp.where(is_first, emb_sum, 0.0).astype(jnp.bfloat16)  40.8 us
    dot_general x12, matrix products, layer_backward(): jnp.einsum('tf,th->fh', hidden, cot_cur, preferred_element_type=jnp.float32)  23.3 us
    dot_general x12, matrix products, layer_backward(): jnp.einsum('th,tf->hf', x_cur, d_pre, preferred_element_type=jnp.float32)  22.1 us
  transfers between devices with their start and end apart: 10, of which 5 were waited for; matrix products, arithmetic and copies ran while one was open for 11% of the time, Pallas kernels for 0%

commit v1 on v0

v1 whole, which is shorter than its diff:
```python
import functools

import jax
import jax.numpy as jnp
from jax import lax
from jax.experimental import pallas as pl
from jax.experimental.pallas import tpu as pltpu
from jax.sharding import PartitionSpec as P

MESH_ID = pl.DeviceIdType.MESH
BF = jnp.bfloat16
F32 = jnp.float32

VOCAB_CHUNK = 768
CHUNKS = 5
HALF_VOCAB = VOCAB_CHUNK * CHUNKS
WEIGHT_UNITS = 6
UNIT_ORDER = (('w', 0), ('e', 0), ('e', 1), ('e', 2), ('e', 3), ('e', 4), ('w', 1), ('w', 2), ('w', 3), ('w', 4), ('w', 5))
LAG_ADD, LAG_SECOND, LAG_LAST = 1, 3, 5


def layer_forward(x_cur, w_in_l, w_out_l):
    pre_act = jnp.dot(x_cur, w_in_l, preferred_element_type=F32).astype(BF)
    hidden = jax.nn.gelu(pre_act.astype(F32)).astype(BF)
    out_x = (x_cur.astype(F32) + jnp.dot(hidden, w_out_l, preferred_element_type=F32)).astype(BF)
    return out_x, pre_act, hidden


def chain_xla(d_out, stored_x, w_in, w_out, stages):
    stage_id = lax.axis_index('pp')
    layers = w_in.shape[0]
    rows = d_out.shape[1]
    x_steps = []
    for step_id in range(stages):
        micro_id = jnp.maximum(stages - 1 - stage_id - step_id, 0)
        x_steps.append(lax.dynamic_index_in_dim(stored_x[0], micro_id, axis=0, keepdims=False))
    x_cur = jnp.concatenate(x_steps, axis=0)
    saved = []
    for layer_id in range(layers):
        out_x, pre_act, hidden = layer_forward(x_cur, w_in[layer_id], w_out[layer_id])
        slope = jax.jvp(jax.nn.gelu, (pre_act.astype(F32),), (jnp.ones(pre_act.shape, F32),))[1]
        saved.append((x_cur, hidden, slope))
        x_cur = out_x
    g_all = [[None] * stages for _ in range(layers)]
    dh_all = [[None] * stages for _ in range(layers)]
    dx_all = []
    cot = d_out[0]
    for step_id in range(stages):
        sl = slice(step_id * rows, (step_id + 1) * rows)
        for layer_id in range(layers - 1, -1, -1):
            g_all[layer_id][step_id] = cot
            d_hidden = lax.dot_general(cot, w_out[layer_id], (((1,), (1,)), ((), ())), preferred_element_type=F32).astype(BF)
            d_pre = (d_hidden.astype(F32) * saved[layer_id][2][sl]).astype(BF)
            dh_all[layer_id][step_id] = d_pre
            back = lax.dot_general(d_pre, w_in[layer_id], (((1,), (1,)), ((), ())), preferred_element_type=F32)
            cot = (cot.astype(F32) + back).astype(BF)
        dx_all.append(cot)
        if step_id < stages - 1:
            cot = lax.ppermute(cot, 'pp', [(sender, sender - 1) for sender in range(1, stages)])
    xs = jnp.stack([s[0] for s in saved])
    hs = jnp.stack([s[1] for s in saved])
    gs = jnp.stack([jnp.concatenate(r, axis=0) for r in g_all])
    dhs = jnp.stack([jnp.concatenate(r, axis=0) for r in dh_all])
    return xs, hs, gs, dhs, jnp.concatenate(dx_all, axis=0)


def ag_events():
    events = [(k, hop) for k in range(CHUNKS) for hop in (1, 2, 3)]
    return sorted(events, key=lambda e: (e[0] + e[1], e[1]))


def comm_kernel(stages, vocab, ids_ref, dx_ref, x_ref, h_ref, g_ref, dh_ref, acc_in, acc_out, acc_emb,
                gin_ref, gout_ref, emb_ref,
                u_in, r0_in, r1_in, r2_in, u_out, r0_out, r1_out, r2_out, u_e, r0_e, r1_e, r2_e,
                ag, dxb, st_in, st_out, st_e, st_t,
                sem_st_in, sem_st_out, sem_st_e, sem_t, s0s, s0r, s1s, s1r, s2s, s2r,
                dxs, dxr, up_s, dn_s, pt_s, col_r, pt_r):
    s = lax.axis_index('pp')
    d = lax.axis_index('dp')
    c = lax.rem(d, 2)
    x = lax.rem(d // 2, 2)
    y = d // 4
    core_peer = d + 1 - 2 * c
    x_peer = d + 2 - 4 * x
    y_peer = d + 4 - 8 * y
    last = stages - 1

    def send(src, dst, ss, rs, target):
        return pltpu.make_async_remote_copy(src_ref=src, dst_ref=dst, send_sem=ss, recv_sem=rs, device_id=target, device_id_type=MESH_ID)

    barrier = pltpu.get_barrier_semaphore()
    for peer in (core_peer, x_peer, y_peer):
        pl.semaphore_signal(barrier, inc=1, device_id=(s, peer), device_id_type=MESH_ID)
    for off in range(1, stages):
        pl.semaphore_signal(barrier, inc=1, device_id=(lax.rem(s + off, stages), d), device_id_type=MESH_ID)

    def in_copy(n):
        unit, yx = n // 4, lax.rem(n, 4)
        slot = lax.rem(n, 2)
        return pltpu.make_async_copy(acc_in.at[unit, pl.ds(yx * 128, 128), :], st_in.at[slot], sem_st_in.at[slot])

    def out_copy(n):
        unit, yx = n // 4, lax.rem(n, 4)
        slot = lax.rem(n, 2)
        return pltpu.make_async_copy(acc_out.at[unit, pl.ds(yx * 512, 512), :], st_out.at[slot], sem_st_out.at[slot])

    part_rows = HALF_VOCAB * 4
    chunk_rows = VOCAB_CHUNK * 4
    tail_rows = vocab * 4 - (part_rows * 2 * stages - chunk_rows)

    def emb_copy(n, act):
        k, half = n // 2, n % 2
        slot = n % 2
        start = pl.multiple_of(s * (2 * part_rows) + half * part_rows + k * chunk_rows, 8)

        def full():
            act(pltpu.make_async_copy(acc_emb.at[pl.ds(start, chunk_rows), :], st_e.at[slot], sem_st_e.at[slot]))

        if k == CHUNKS - 1 and half == 1:
            @pl.when(s == last)
            def _():
                act(pltpu.make_async_copy(acc_emb.at[pl.ds(vocab * 4 - tail_rows, tail_rows), :],
                                          st_e.at[slot, pl.ds(0, tail_rows), :], sem_st_e.at[slot]))

            @pl.when(s != last)
            def _():
                full()
        else:
            full()

    for n in range(2):
        in_copy(jnp.int32(n)).start()
        out_copy(jnp.int32(n)).start()
        emb_copy(n, lambda cp: cp.start())

    pl.semaphore_wait(barrier, 3 + stages - 1)

    @pl.when(s == 0)
    def _():
        for z in range(1, stages):
            send(dx_ref, dxb, dxs.at[z], dxr, (z, d)).start()
        for q in range(4):
            dxb[q] = dx_ref[q]

    def weight_produce(unit):
        layer = unit // 2
        if unit % 2 == 0:
            def body(yx, carry):
                n = 4 * layer + yx
                slot = lax.rem(n, 2)
                in_copy(n).wait()
                lhs = x_ref[layer, :, pl.ds(pl.multiple_of(yx * 128, 128), 128)]
                for col in range(4):
                    cs = slice(col * 512, (col + 1) * 512)
                    new = lax.dot_general(lhs, dh_ref[layer, :, cs], (((0,), (0,)), ((), ())), preferred_element_type=F32)
                    tot = (st_in[slot, :, cs] + new).astype(BF)
                    u_in[layer, yx, 0, :, cs] = tot[:64]
                    u_in[layer, yx, 1, :, cs] = tot[64:]

                @pl.when(n + 2 < 12)
                def _():
                    in_copy(n + 2).start()
                return carry
        else:
            def body(yx, carry):
                n = 4 * layer + yx
                slot = lax.rem(n, 2)
                out_copy(n).wait()
                for part in range(4):
                    rows = pl.ds(part * 128, 128)
                    lhs = h_ref[layer, :, pl.ds(pl.multiple_of(yx * 512 + part * 128, 128), 128)]
                    new = lax.dot_general(lhs, g_ref[layer], (((0,), (0,)), ((), ())), preferred_element_type=F32)
                    tot = (st_out[slot, rows, :] + new).astype(BF)
                    u_out[layer, yx, part // 2, pl.ds((part % 2) * 128, 128), :] = tot

                @pl.when(n + 2 < 12)
                def _():
                    out_copy(n + 2).start()
                return carry
        lax.fori_loop(0, 4, body, 0)

    def emb_produce(k):
        if k == 0:
            @pl.when(s > 0)
            def _():
                send(dx_ref, dxb, dxs.at[0], dxr, (0, d)).wait_recv()
        for half in range(2):
            n = 2 * k + half
            emb_copy(n, lambda cp: cp.wait())
            base = s * (2 * HALF_VOCAB) + half * HALF_VOCAB + k * VOCAB_CHUNK
            hot = (lax.broadcasted_iota(jnp.int32, (VOCAB_CHUNK, 128), 0) + base == ids_ref[...]).astype(F32).astype(BF)

            def body(q, carry):
                new = jnp.dot(hot, dxb[q], preferred_element_type=F32)
                old = st_e[n % 2, pl.ds(q, VOCAB_CHUNK, stride=4), :]
                u_e[k, q, half] = (old + new).astype(BF)
                return carry
            lax.fori_loop(0, 4, body, 0)
            if n + 2 < 2 * CHUNKS:
                emb_copy(n + 2, lambda cp: cp.start())

    def unit_bufs(kind, i):
        if kind == 'e':
            return u_e.at[i], r0_e.at[i], r1_e.at[i], r2_e.at[i], VOCAB_CHUNK
        if i % 2 == 0:
            return u_in.at[i // 2], r0_in.at[i // 2], r1_in.at[i // 2], r2_in.at[i // 2], 64
        return u_out.at[i // 2], r0_out.at[i // 2], r1_out.at[i // 2], r2_out.at[i // 2], 256

    def add_into(u, idx, r, ridx):
        u[idx] = u[idx] + r[ridx]

    def core_send(pos):
        u, r0, r1, r2, rows = unit_bufs(*UNIT_ORDER[pos])
        return send(u.at[:, 1 - c], r0, s0s.at[pos], s0r.at[pos], (s, core_peer))

    def first_send(pos):
        u, r0, r1, r2, rows = unit_bufs(*UNIT_ORDER[pos])
        if pos % 2 == 0:
            return [send(u.at[2 * j + 1 - x, c], r1.at[j], s1s.at[pos, j], s1r.at[pos, j], (s, x_peer)) for j in range(2)]
        return [send(u.at[2 * (1 - y) + j, c], r1.at[j], s1s.at[pos, j], s1r.at[pos, j], (s, y_peer)) for j in range(2)]

    def second_send(pos):
        u, r0, r1, r2, rows = unit_bufs(*UNIT_ORDER[pos])
        if pos % 2 == 0:
            return send(u.at[2 * (1 - y) + x, c], r2, s2s.at[pos], s2r.at[pos], (s, y_peer))
        return send(u.at[2 * y + 1 - x, c], r2, s2s.at[pos], s2r.at[pos], (s, x_peer))

    def stage_produce(pos):
        kind, i = UNIT_ORDER[pos]
        if kind == 'w':
            weight_produce(i)
        else:
            emb_produce(i)
        core_send(pos).start()

    def stage_add(pos):
        u, r0, r1, r2, rows = unit_bufs(*UNIT_ORDER[pos])
        core_send(pos).wait_recv()
        sends = first_send(pos)
        order = ([2 * j + 1 - x for j in range(2)] + [2 * j + x for j in range(2)]) if pos % 2 == 0 else \
                ([2 * (1 - y) + j for j in range(2)] + [2 * y + j for j in range(2)])
        for j, blk in enumerate(order):
            u[blk, c] = u[blk, c] + r0[blk]
            if j < 2:
                sends[j].start()

    def stage_second(pos):
        u, r0, r1, r2, rows = unit_bufs(*UNIT_ORDER[pos])
        for cp in first_send(pos):
            cp.wait_recv()
        if pos % 2 == 0:
            far, near = (2 * (1 - y) + x, 1 - y), (2 * y + x, y)
        else:
            far, near = (2 * y + 1 - x, 1 - x), (2 * y + x, x)
        u[far[0], c] = u[far[0], c] + r1[far[1]]
        second_send(pos).start()
        u[near[0], c] = u[near[0], c] + r1[near[1]]

    def col_send(z, k, sem, target_s):
        piece = ag.at[2 * z + c, k]
        return send(piece, piece, sem.at[z, k], col_r.at[z, k], (target_s, d))

    def part_send(z, k):
        piece = ag.at[2 * z + c, k]
        return send(piece, piece, pt_s.at[z, k], pt_r.at[z, k], (s, core_peer))

    counter = [0]
    sel = (lax.broadcasted_iota(jnp.int32, (64, 128), 1) == lax.broadcasted_iota(jnp.int32, (64, 128), 0) + 64 * c).astype(F32).astype(BF)

    def out_copy_t(slot, p, k):
        start = pl.multiple_of(p * HALF_VOCAB + k * VOCAB_CHUNK, 128)
        return pltpu.make_async_copy(st_t.at[slot], emb_ref.at[:, pl.ds(start, VOCAB_CHUNK)], sem_t.at[slot])

    def emit(p, k):
        st_t[k, p] = lax.dot_general(sel, ag[p, k], (((1,), (1,)), ((), ())), preferred_element_type=F32).astype(BF)
        pltpu.make_async_copy(st_t.at[k, p], emb_ref.at[:, pl.ds(pl.multiple_of(p * HALF_VOCAB + k * VOCAB_CHUNK, 128), VOCAB_CHUNK)],
                              sem_t.at[k, p]).start()

    def have_piece(z, k, go_up, go_down):
        if go_up:
            @pl.when(s < last)
            def _():
                col_send(z, k, up_s, s + 1).start()
        if go_down:
            @pl.when(s > 0)
            def _():
                col_send(z, k, dn_s, s - 1).start()
        part_send(z, k).start()
        emit(2 * z + c, k)

    def stage_last(pos):
        kind, i = UNIT_ORDER[pos]
        u, r0, r1, r2, rows = unit_bufs(kind, i)
        second_send(pos).wait_recv()
        mine = 2 * y + x
        if kind == 'e':
            ag[2 * s + c, i] = u[mine, c] + r2[...]
            have_piece(s, i, True, True)
        else:
            tot = (u[mine, c].astype(F32) + r2[...].astype(F32))
            if i % 2 == 0:
                gin_ref[i // 2] = tot
            else:
                gout_ref[i // 2] = tot

    def part_event(z, k):
        part_send(z, k).wait_recv()
        emit(2 * z + 1 - c, k)

    def hop_event(k, hop):
        @pl.when(s - hop >= 0)
        def _():
            z = jnp.maximum(s - hop, 0)
            col_send(z, k, up_s, s).wait_recv()
            have_piece(z, k, True, False)

        @pl.when(s + hop <= last)
        def _():
            z = jnp.minimum(s + hop, last)
            col_send(z, k, dn_s, s).wait_recv()
            have_piece(z, k, False, True)

    events = ag_events()
    total = len(UNIT_ORDER)
    for tick in range(total + LAG_LAST):
        if tick < total:
            stage_produce(tick)
        if 0 <= tick - LAG_ADD < total:
            stage_add(tick - LAG_ADD)
        if 0 <= tick - LAG_SECOND < total:
            stage_second(tick - LAG_SECOND)
        if 0 <= tick - LAG_LAST < total:
            stage_last(tick - LAG_LAST)
        if tick >= 8:
            for _ in range(2):
                if events and events[0][0] <= tick - LAG_LAST - 1:
                    hop_event(*events.pop(0))
    while events:
        hop_event(*events.pop(0))

    def drain_part(i, carry):
        part_event(i // CHUNKS, lax.rem(i, CHUNKS))
        return carry
    lax.fori_loop(0, stages * CHUNKS, drain_part, 0)

    for pos in range(total):
        core_send(pos).wait_send()
        for cp in first_send(pos):
            cp.wait_send()
        second_send(pos).wait_send()

    @pl.when(s == 0)
    def _():
        for z in range(1, stages):
            send(dx_ref, dxb, dxs.at[z], dxr, (z, d)).wait_send()

    def drain(i, carry):
        z, k = i // CHUNKS, lax.rem(i, CHUNKS)
        part_send(z, k).wait_send()

        @pl.when((z <= s) & (s < last))
        def _():
            col_send(z, k, up_s, jnp.minimum(s + 1, last)).wait_send()

        @pl.when((z >= s) & (s > 0))
        def _():
            col_send(z, k, dn_s, jnp.maximum(s - 1, 0)).wait_send()
        for core in range(2):
            pltpu.make_async_copy(st_t.at[k, 2 * z + core], emb_ref.at[:, pl.ds(0, VOCAB_CHUNK)], sem_t.at[k, 2 * z + core]).wait()
        return carry
    lax.fori_loop(0, stages * CHUNKS, drain, 0)


def solution(mesh):
    stages = mesh.shape['pp']
    replicas = mesh.shape['dp']

    def device_body(tok_ids, d_out, stored_x, w_in, w_out, acc_in, acc_out, acc_emb):
        layers, hid, ff = w_in.shape
        vocab = acc_emb.shape[1]
        xs, hs, gs, dhs, dx = chain_xla(d_out, stored_x, w_in, w_out, stages)
        rows = dx.shape[0]
        ids = tok_ids[::-1].reshape(1, rows)
        dx_q = dx.reshape(rows, 4, 128).transpose(1, 0, 2)
        v = pltpu.VMEM
        dma = pltpu.SemaphoreType.DMA
        units = len(UNIT_ORDER)
        vm = pl.BlockSpec(memory_space=pltpu.VMEM)
        hbm = pl.BlockSpec(memory_space=pltpu.HBM)
        gin, gout, emb = pl.pallas_call(
            functools.partial(comm_kernel, stages, vocab),
            out_shape=(jax.ShapeDtypeStruct((layers, hid // 8, ff), F32), jax.ShapeDtypeStruct((layers, ff // 8, hid), F32),
                       jax.ShapeDtypeStruct((64, HALF_VOCAB * 2 * stages), BF)),
            in_specs=[vm] * 6 + [hbm] * 3,
            out_specs=(vm, vm, hbm),
            scratch_shapes=[
                v((layers, 4, 2, 64, ff), BF), v((layers, 4, 64, ff), BF), v((layers, 2, 64, ff), BF), v((layers, 64, ff), BF),
                v((layers, 4, 2, 256, hid), BF), v((layers, 4, 256, hid), BF), v((layers, 2, 256, hid), BF), v((layers, 256, hid), BF),
                v((CHUNKS, 4, 2, VOCAB_CHUNK, 128), BF), v((CHUNKS, 4, VOCAB_CHUNK, 128), BF), v((CHUNKS, 2, VOCAB_CHUNK, 128), BF), v((CHUNKS, VOCAB_CHUNK, 128), BF),
                v((2 * stages, CHUNKS, VOCAB_CHUNK, 128), BF), v((4, rows, 128), BF),
                v((2, 128, ff), F32), v((2, 512, hid), F32), v((2, VOCAB_CHUNK * 4, 128), F32), v((CHUNKS, 2 * stages, 64, VOCAB_CHUNK), BF),
                dma((2,)), dma((2,)), dma((2,)), dma((CHUNKS, 2 * stages)),
                dma((units,)), dma((units,)), dma((units, 2)), dma((units, 2)), dma((units,)), dma((units,)),
                dma((stages,)), dma, dma((stages, CHUNKS)), dma((stages, CHUNKS)), dma((stages, CHUNKS)), dma((stages, CHUNKS)), dma((stages, CHUNKS)),
            ],
            compiler_params=pltpu.CompilerParams(collective_id=0, has_side_effects=True, vmem_limit_bytes=67043328),
            name='reduce_exchange',
        )(ids, dx_q, xs, hs, gs, dhs, acc_in.reshape(layers, hid, ff), acc_out.reshape(layers, ff, hid), acc_emb.reshape(vocab * 4, 128))
        scale = 1.0 / replicas
        grad_emb = (emb[:, :vocab].astype(F32) * scale).T
        return gin * scale, gout * scale, grad_emb

    return jax.shard_map(device_body, mesh=mesh, in_specs=(P(None, 'dp'), P('pp', 'dp', None), P('pp', None, 'dp', None), P('pp', None, None), P('pp', None, None), P('pp', 'dp', None, None), P('pp', 'dp', None, None), P('dp', None, None)), out_specs=(P('pp', 'dp', None), P('pp', 'dp', None), P(None, 'dp')), check_vma=False)
```

time: 1040 us -> 188 us (0.18); the launches traced: 1030 us -> 186 us
  waiting for transfers between devices: 734 us -> 0.99 us
  Pallas kernels: 0 us -> 119 us
  local copies, waits for them, and re-layouts: 97.5 us -> 3.84 us
  matrix products: 111 us -> 35.2 us
  other arithmetic: 53.7 us -> 15.1 us
  between operations: 15.4 us -> 1.43 us
    ppermute x6 -> x3, waiting for transfers between devices: 349 us -> 0.99 us  [chain_xla(): lax.ppermute(cot, 'pp', [(sender, sender - 1) for sender in range(1, stag...]
    reduce_scatter x3 -> x0, waiting for transfers between devices: 312 us -> none  [the longest x1 186 us: device_body(): summed = lax.psum_scatter(own_piece, 'dp', scatter_dimension=1, tiled=True)]
    pallas_call x0 -> x1, Pallas kernels: none -> 119 us  [device_body(): pl.pallas_call(functools.partial(comm_kernel, stages, vocab), out_shape=(...]
    dot_general x68 -> x29, matrix products: 111 us -> 35.2 us  [the longest x12 14.1 us: chain_xla(): lax.dot_general(d_pre, w_in[layer_id], (((1,), (1,)), ((), ())), preferre...]
    all_gather x1 -> x0, waiting for transfers between devices: 72.4 us -> none  [device_body(): gathered = lax.all_gather(summed[:, 0, :], 'pp', axis=1)]
    unnamed x157 -> x80, local copies, waits for them, and re-layouts: 45.3 us -> 2.23 us
    convert_element_type x1 -> x0, local copies, waits for them, and re-layouts: 40.8 us -> none  [device_body(): jnp.where(is_first, emb_sum, 0.0).astype(jnp.bfloat16)]
    scatter-add x1 -> x0, other arithmetic: 15.9 us -> none  [cooldown_local(): emb_sum = acc_emb[0].at[ids_steps].add(jnp.where(is_first, dx_all, 0.0))]
  transfers between devices with their start and end apart: 10 -> 3, of which waited for: 5 -> 1; matrix products, arithmetic and copies ran while one was open for 11% -> 1% of each run, Pallas kernels for 0% -> 0%
where the time goes in v1:
time: 188 us; the launch traced here: 186 us
  Pallas kernels  119 us (63%)
  matrix products  35.2 us (19%)
  other arithmetic  15.1 us (8%)
  starting transfers between devices  9.66 us (5%)
  local copies, waits for them, and re-layouts  3.84 us (2%)
    pallas_call x1, Pallas kernels, device_body(): pl.pallas_call(functools.partial(comm_kernel, stages, vocab), out_shape=(...  119 us
    dot_general x12, matrix products, chain_xla(): lax.dot_general(d_pre, w_in[layer_id], (((1,), (1,)), ((), ())), preferre...  14.1 us
    dot_general x12, matrix products, chain_xla(): lax.dot_general(cot, w_out[layer_id], (((1,), (1,)), ((), ())), preferred...  13.5 us
    ppermute x3, starting transfers between devices, chain_xla(): lax.ppermute(cot, 'pp', [(sender, sender - 1) for sender in range(1, stag...  9.66 us
    dot_general x3, matrix products, layer_forward(): pre_act = jnp.dot(x_cur, w_in_l, preferred_element_type=F32).astype(BF)  4.65 us
    mul x2, other arithmetic, device_body(): return (gin * scale, gout * scale, grad_emb)  4.19 us
  transfers between devices with their start and end apart: 3, of which 1 were waited for; matrix products, arithmetic and copies ran while one was open for 1% of the time, Pallas kernels for 0%

profile of v1, /device:TPU:25, one launch (start us, length us, event | category | flops | bytes accessed | tf_op | source)
XLA Modules:
  0.0 185.6 jit_solution(11206488529521233129)
XLA Ops:
  0.7 1.0 dynamic-slice_bitcast_fusion.3
  1.6 2.5 %fusion.2 = f32[128,2048]{1,0:T(8,128)S(1)} fusion(bf16[3,512,2048]{2,1,0:T(8,128)(2,1)} %param.11, bf16[32,512]{1,0:T(8,128)(2,1)S(1)} %get-tuple-element.17, bf16[32,512]{1,0:T(8,128)(2,1)S(1)} %get-tuple-element.18, bf16[32,512]{1,0:T(8,128)(2,1)S(1)} %get-tuple-element.16, bf16[32,512]{1,0:T(8,128)(2,1)S(1)} %get-tuple-element.15), kind=kOutput, calls=%fused_computation.6 | convolution fusion | flops 269484032 | bytes 3276800 | tf_op jit(solution)/shard_map/dot_general | solution.py:23
  4.2 2.3 %fusion.95 = bf16[128,512]{1,0:T(8,128)(2,1)S(1)} fusion(bf16[3,2048,512]{2,1,0:T(8,128)(2,1)} %param.12, bf16[32,512]{1,0:T(8,128)(2,1)S(1)} %get-tuple-element.17, bf16[32,512]{1,0:T(8,128)(2,1)S(1)} %get-tuple-element.18, bf16[32,512]{1,0:T(8,128)(2,1)S(1)} %get-tuple-element.16, bf16[32,512]{1,0:T(8,128)(2,1)S(1)} %get-tuple-element.15, ...), kind=kOutput, calls=%fused_computation.113 | convolution fusion | flops 271450112 | bytes 3407872 | tf_op jit(solution)/shard_map/dot_general | solution.py:25
  7.0 0.6 fusion.92
  7.6 0.6 fusion.193
  8.2 1.7 fusion.189
  9.9 0.7 fusion.38
  10.7 0.7 fusion.116
  11.4 0.7 fusion.35
  12.2 0.7 fusion.119
  12.9 0.7 fusion.32
  13.6 0.7 fusion.131
  14.4 2.1 %collective-permute-start = (bf16[32,512]{1,0:T(8,128)(2,1)S(1)}, bf16[32,512]{1,0:T(8,128)(2,1)S(1)}, u32[]{:S(2)}, u32[]{:S(2)}) collective-permute-start(bf16[32,512]{1,0:T(8,128)(2,1)S(1)} %fusion.131), channel_id=1, source_target_pairs={{8,0},{16,8},{24,16},{9,1},{17,9},{25,17},{10,2},{18,10},{26,18},{... | collective-permute-start | bytes 98312 | tf_op jit(solution)/shard_map/ppermute | solution.py:59
  16.5 1.3 pad_maximum_fusion.h_ref
  17.8 0.7 fusion.29
  18.5 0.6 copy-done.9
  19.2 0.7 add_convert_fusion.5
  19.9 0.7 fusion.26
  20.7 0.7 add_convert_fusion.4
  21.4 0.7 fusion.23
  22.2 0.7 fusion.128
  22.9 3.3 %collective-permute-start.1 = (bf16[32,512]{1,0:T(8,128)(2,1)S(1)}, bf16[32,512]{1,0:T(8,128)(2,1)S(1)}, u32[]{:S(2)}, u32[]{:S(2)}) collective-permute-start(bf16[32,512]{1,0:T(8,128)(2,1)S(1)} %fusion.128), channel_id=1, source_target_pairs={{8,0},{16,8},{24,16},{9,1},{17,9},{25,17},{10,2},{18,10},{26,18},{... | collective-permute-start | bytes 98312 | tf_op jit(solution)/shard_map/ppermute | solution.py:59
  26.3 1.0 collective-permute-done.1
  27.3 0.7 fusion.20
  28.0 0.6 copy-done.13
  28.7 0.7 add_convert_fusion.3
  29.4 0.7 fusion.17
  30.2 0.7 copy-done.11
  30.8 0.7 add_convert_fusion.2
  31.6 0.7 fusion.14
  32.3 1.4 fusion.125
  33.7 4.2 %collective-permute-start.2 = (bf16[32,512]{1,0:T(8,128)(2,1)}, bf16[32,512]{1,0:T(8,128)(2,1)}, u32[]{:S(2)}, u32[]{:S(2)}) collective-permute-start(bf16[32,512]{1,0:T(8,128)(2,1)} %fusion.125), channel_id=1, source_target_pairs={{8,0},{16,8},{24,16},{9,1},{17,9},{25,17},{10,2},{18,10},{26,18},{... | collective-permute-start | bytes 98312 | tf_op jit(solution)/shard_map/ppermute | solution.py:59
  37.9 0.8 pad_maximum_fusion.2.x_ref
  38.7 0.6 reshape.29.ids_ref
  39.4 2.4 %fusion.11 = bf16[32,2048]{1,0:T(8,128)(2,1)S(1)} fusion(bf16[32,512]{1,0:T(8,128)(2,1)} %collective-permute-done.2, bf16[3,2048,512]{2,1,0:T(8,128)(2,1)} %param.12, f32[128,2048]{1,0:T(8,128)S(1)} %get-tuple-element.14), kind=kOutput, calls=%fused_computation.18 | convolution fusion | flops 67371008 | bytes 2523136 | tf_op jit(solution)/shard_map/dot_general | solution.py:52
  41.8 2.3 %add_convert_fusion.1 = bf16[32,512]{1,0:T(8,128)(2,1)S(1)} fusion(bf16[32,512]{1,0:T(8,128)(2,1)} %collective-permute-done.2, bf16[32,2048]{1,0:T(8,128)(2,1)S(1)} %fusion.11, bf16[3,512,2048]{2,1,0:T(8,128)(2,1)} %param.11), kind=kOutput, calls=%fused_computation.199 | convolution fusion | flops 67158016 | bytes 2293760 | tf_op jit(solution)/shard_map/dot_general | solution.py:55
  44.2 2.4 %fusion.8 = bf16[32,2048]{1,0:T(8,128)(2,1)S(1)} fusion(bf16[32,512]{1,0:T(8,128)(2,1)S(1)} %add_convert_fusion.1, bf16[3,2048,512]{2,1,0:T(8,128)(2,1)} %param.12, f32[128,2048]{1,0:T(8,128)S(1)} %get-tuple-element.12), kind=kOutput, calls=%fused_computation.14 | convolution fusion | flops 67371008 | bytes 2523136 | tf_op jit(solution)/shard_map/dot_general | solution.py:52
  46.6 2.3 %add_convert_fusion = bf16[32,512]{1,0:T(8,128)(2,1)S(1)} fusion(bf16[32,512]{1,0:T(8,128)(2,1)S(1)} %add_convert_fusion.1, bf16[32,2048]{1,0:T(8,128)(2,1)S(1)} %fusion.8, bf16[3,512,2048]{2,1,0:T(8,128)(2,1)} %param.11), kind=kOutput, calls=%fused_computation.198 | convolution fusion | flops 67158016 | bytes 2293760 | tf_op jit(solution)/shard_map/dot_general | solution.py:55
  49.1 2.3 %fusion.5 = bf16[32,2048]{1,0:T(8,128)(2,1)S(1)} fusion(bf16[32,512]{1,0:T(8,128)(2,1)S(1)} %add_convert_fusion, bf16[3,2048,512]{2,1,0:T(8,128)(2,1)} %param.12, f32[128,2048]{1,0:T(8,128)S(1)} %get-tuple-element.19), kind=kOutput, calls=%fused_computation.10 | convolution fusion | flops 67371008 | bytes 2523136 | tf_op jit(solution)/shard_map/dot_general | solution.py:52
  51.5 2.3 %fusion.122 = bf16[32,512]{1,0:T(8,128)(2,1)S(1)} fusion(bf16[32,2048]{1,0:T(8,128)(2,1)S(1)} %fusion.5, bf16[3,512,2048]{2,1,0:T(8,128)(2,1)} %param.11, bf16[32,512]{1,0:T(8,128)(2,1)S(1)} %add_convert_fusion), kind=kOutput, calls=%fused_computation.122 | convolution fusion | flops 67158016 | bytes 2293760 | tf_op jit(solution)/shard_map/dot_general | solution.py:55
  53.9 1.5 bitcast_bitcast_fusion.dx_ref
  55.4 1.3 pad_maximum_fusion.1.dh_ref
  56.7 0.8 maximum_bitcast_fusion.6
  57.5 0.8 pad_maximum_fusion.3.g_ref
  58.3 119.4 %reduce_exchange.1 = (f32[3,64,2048]{2,1,0:T(8,128)}, f32[3,256,512]{2,1,0:T(8,128)}, bf16[64,30720]{1,0:T(8,128)(2,1)}) custom-call(s32[1,128]{1,0:T(1,128)} %reshape.29.ids_ref, bf16[4,128,128]{2,1,0:T(8,128)(2,1)} %bitcast_bitcast_fusion.dx_ref, bf16[3,128,512]{2,1,0:T(8,128)(2,1)} %pad_maximum_fusion.2.x_ref, ...), custom_call_target="tpu_custom_call" | custom-call | tf_op jit(solution)/shard_map/reduce_exchange/pallas_call | solution.py:390
  177.7 2.9 %broadcast_multiply_fusion.1 = f32[3,64,2048]{2,1,0:T(8,128)} fusion(f32[3,64,2048]{2,1,0:T(8,128)} %get-tuple-element.6), kind=kLoop, calls=%fused_computation.185 | loop fusion | flops 393216 | bytes 3145728 | tf_op jit(solution)/shard_map/mul | solution.py:411
  180.6 1.3 broadcast_multiply_fusion
  181.9 3.7 %multiply_bitcast_fusion = f32[30522,64]{0,1:T(8,128)} fusion(bf16[64,30720]{1,0:T(8,128)(2,1)S(1)} %copy-done), kind=kLoop, calls=%fused_computation | loop fusion | flops 3906816 | bytes 11720448 | tf_op jit(solution)/shard_map/transpose | solution.py:410
  (88 shorter events, 0.9 us)
Async XLA Ops:
  0.6 5.9 %copy-start.1 = (bf16[3,512,2048]{2,1,0:T(8,128)(2,1)S(1)}, bf16[3,512,2048]{2,1,0:T(8,128)(2,1)}, u32[]{:S(2)}) copy-start(bf16[3,512,2048]{2,1,0:T(8,128)(2,1)} %param.11) | copy-start | bytes 18874372
  1.6 5.4 %slice-start = ((s8[6291456]{0:T(1024)(128)(4,1)}), s8[4194304]{0:T(1024)(128)(4,1)S(1)}, s32[]{:S(2)}) async-start(s8[6291456]{0:T(1024)(128)(4,1)} %bitcast.181), calls=%async_computation | async-start | bytes 8388608
  4.2 2.8 %slice-start.1 = ((s8[6291456]{0:T(1024)(128)(4,1)}), s8[2097152]{0:T(1024)(128)(4,1)S(1)}, s32[]{:S(2)}) async-start(s8[6291456]{0:T(1024)(128)(4,1)} %bitcast.181), calls=%async_computation.1 | async-start | bytes 4194304
  8.2 1.7 copy-start.15
  10.7 1.5 copy-start.3
  11.4 1.5 copy-start.23
  12.9 1.5 copy-start.19
  14.4 4.1 %copy-start.33 = (bf16[32,512]{1,0:T(8,128)(2,1)}, bf16[32,512]{1,0:T(8,128)(2,1)S(1)}, u32[]{:S(2)}) copy-start(bf16[32,512]{1,0:T(8,128)(2,1)S(1)} %fusion.131) | copy-start | bytes 98308
  14.4 3.4 %collective-permute-start = (bf16[32,512]{1,0:T(8,128)(2,1)S(1)}, bf16[32,512]{1,0:T(8,128)(2,1)S(1)}, u32[]{:S(2)}, u32[]{:S(2)}) collective-permute-start(bf16[32,512]{1,0:T(8,128)(2,1)S(1)} %fusion.131), channel_id=1, source_target_pairs={{8,0},{16,8},{24,16},{9,1},{17,9},{25,17},{10,2},{18,10},{26,18},{... | collective-permute-start | bytes 98312 | tf_op jit(solution)/shard_map/ppermute | solution.py:59
  17.8 2.1 %copy-start.17 = (bf16[32,512]{1,0:T(8,128)(2,1)}, bf16[32,512]{1,0:T(8,128)(2,1)S(1)}, u32[]{:S(2)}) copy-start(bf16[32,512]{1,0:T(8,128)(2,1)S(1)} %collective-permute-done) | copy-start | bytes 98308
  18.5 0.7 copy-start.9
  19.9 1.5 copy-start.27
  20.7 1.5 copy-start.5
  21.4 0.7 copy-start.25
  22.9 6.5 %copy-start.35 = (bf16[32,512]{1,0:T(8,128)(2,1)}, bf16[32,512]{1,0:T(8,128)(2,1)S(1)}, u32[]{:S(2)}) copy-start(bf16[32,512]{1,0:T(8,128)(2,1)S(1)} %fusion.128) | copy-start | bytes 98308
  22.9 4.3 %collective-permute-start.1 = (bf16[32,512]{1,0:T(8,128)(2,1)S(1)}, bf16[32,512]{1,0:T(8,128)(2,1)S(1)}, u32[]{:S(2)}, u32[]{:S(2)}) collective-permute-start(bf16[32,512]{1,0:T(8,128)(2,1)S(1)} %fusion.128), channel_id=1, source_target_pairs={{8,0},{16,8},{24,16},{9,1},{17,9},{25,17},{10,2},{18,10},{26,18},{... | collective-permute-start | bytes 98312 | tf_op jit(solution)/shard_map/ppermute | solution.py:59
  27.3 2.1 %copy-start.21 = (bf16[32,512]{1,0:T(8,128)(2,1)}, bf16[32,512]{1,0:T(8,128)(2,1)S(1)}, u32[]{:S(2)}) copy-start(bf16[32,512]{1,0:T(8,128)(2,1)S(1)} %collective-permute-done.1) | copy-start | bytes 98308
  28.0 0.7 copy-start.13
  29.4 2.1 %copy-start.31 = (bf16[32,512]{1,0:T(8,128)(2,1)}, bf16[32,512]{1,0:T(8,128)(2,1)S(1)}, u32[]{:S(2)}) copy-start(bf16[32,512]{1,0:T(8,128)(2,1)S(1)} %add_convert_fusion.3) | copy-start | bytes 98308
  30.1 0.7 copy-start.11
  31.6 2.1 %copy-start.29 = (bf16[32,512]{1,0:T(8,128)(2,1)}, bf16[32,512]{1,0:T(8,128)(2,1)S(1)}, u32[]{:S(2)}) copy-start(bf16[32,512]{1,0:T(8,128)(2,1)S(1)} %add_convert_fusion.2) | copy-start | bytes 98308
  32.3 1.4 copy-start.7
  32.3 6.4 %copy-start.37 = (s32[4,32]{1,0:T(4,128)S(1)}, s32[4,32]{1,0:T(4,128)}, u32[]{:S(2)}) copy-start(s32[4,32]{1,0:T(4,128)} %param.8) | copy-start | bytes 1540
  33.7 5.7 %collective-permute-start.2 = (bf16[32,512]{1,0:T(8,128)(2,1)}, bf16[32,512]{1,0:T(8,128)(2,1)}, u32[]{:S(2)}, u32[]{:S(2)}) collective-permute-start(bf16[32,512]{1,0:T(8,128)(2,1)} %fusion.125), channel_id=1, source_target_pairs={{8,0},{16,8},{24,16},{9,1},{17,9},{25,17},{10,2},{18,10},{26,18},{... | collective-permute-start | bytes 98312 | tf_op jit(solution)/shard_map/ppermute | solution.py:59
  39.3 2.4 %copy-start.4 = (bf16[32,2048]{1,0:T(8,128)(2,1)S(1)}, bf16[32,2048]{1,0:T(8,128)(2,1)}, u32[]{:S(2)}) copy-start(bf16[32,2048]{1,0:T(8,128)(2,1)} %copy-done.3) | copy-start | bytes 393220
  39.3 2.4 %copy-start.10 = (bf16[32,2048]{1,0:T(8,128)(2,1)S(1)}, bf16[32,2048]{1,0:T(8,128)(2,1)}, u32[]{:S(2)}) copy-start(bf16[32,2048]{1,0:T(8,128)(2,1)} %copy-done.9) | copy-start | bytes 393220
  39.4 2.4 %copy-start.14 = (bf16[32,2048]{1,0:T(8,128)(2,1)S(1)}, bf16[32,2048]{1,0:T(8,128)(2,1)}, u32[]{:S(2)}) copy-start(bf16[32,2048]{1,0:T(8,128)(2,1)} %copy-done.13) | copy-start | bytes 393220
  44.1 4.8 %copy-start.6 = (bf16[32,2048]{1,0:T(8,128)(2,1)S(1)}, bf16[32,2048]{1,0:T(8,128)(2,1)}, u32[]{:S(2)}) copy-start(bf16[32,2048]{1,0:T(8,128)(2,1)} %copy-done.5) | copy-start | bytes 393220
  44.2 4.8 %copy-start.12 = (bf16[32,2048]{1,0:T(8,128)(2,1)S(1)}, bf16[32,2048]{1,0:T(8,128)(2,1)}, u32[]{:S(2)}) copy-start(bf16[32,2048]{1,0:T(8,128)(2,1)} %copy-done.11) | copy-start | bytes 393220
  46.5 2.5 %copy-start.24 = (bf16[32,512]{1,0:T(8,128)(2,1)S(1)}, bf16[32,512]{1,0:T(8,128)(2,1)}, u32[]{:S(2)}) copy-start(bf16[32,512]{1,0:T(8,128)(2,1)} %copy-done.23) | copy-start | bytes 98308
  46.5 2.5 %copy-start.28 = (bf16[32,512]{1,0:T(8,128)(2,1)S(1)}, bf16[32,512]{1,0:T(8,128)(2,1)}, u32[]{:S(2)}) copy-start(bf16[32,512]{1,0:T(8,128)(2,1)} %copy-done.27) | copy-start | bytes 98308
  46.6 2.5 %copy-start.32 = (bf16[32,512]{1,0:T(8,128)(2,1)S(1)}, bf16[32,512]{1,0:T(8,128)(2,1)}, u32[]{:S(2)}) copy-start(bf16[32,512]{1,0:T(8,128)(2,1)} %copy-done.31) | copy-start | bytes 98308
  48.9 2.5 %copy-start.20 = (bf16[32,512]{1,0:T(8,128)(2,1)S(1)}, bf16[32,512]{1,0:T(8,128)(2,1)}, u32[]{:S(2)}) copy-start(bf16[32,512]{1,0:T(8,128)(2,1)} %copy-done.19) | copy-start | bytes 98308
  48.9 2.5 %copy-start.26 = (bf16[32,512]{1,0:T(8,128)(2,1)S(1)}, bf16[32,512]{1,0:T(8,128)(2,1)}, u32[]{:S(2)}) copy-start(bf16[32,512]{1,0:T(8,128)(2,1)} %copy-done.25) | copy-start | bytes 98308
  48.9 2.5 %copy-start.30 = (bf16[32,512]{1,0:T(8,128)(2,1)S(1)}, bf16[32,512]{1,0:T(8,128)(2,1)}, u32[]{:S(2)}) copy-start(bf16[32,512]{1,0:T(8,128)(2,1)} %copy-done.29) | copy-start | bytes 98308
  49.1 4.8 %copy-start.8 = (bf16[32,2048]{1,0:T(8,128)(2,1)S(1)}, bf16[32,2048]{1,0:T(8,128)(2,1)}, u32[]{:S(2)}) copy-start(bf16[32,2048]{1,0:T(8,128)(2,1)} %copy-done.7) | copy-start | bytes 393220
  51.5 2.5 %copy-start.34 = (bf16[32,512]{1,0:T(8,128)(2,1)S(1)}, bf16[32,512]{1,0:T(8,128)(2,1)}, u32[]{:S(2)}) copy-start(bf16[32,512]{1,0:T(8,128)(2,1)} %copy-done.33) | copy-start | bytes 98308
  51.5 2.5 %copy-start.36 = (bf16[32,512]{1,0:T(8,128)(2,1)S(1)}, bf16[32,512]{1,0:T(8,128)(2,1)}, u32[]{:S(2)}) copy-start(bf16[32,512]{1,0:T(8,128)(2,1)} %copy-done.35) | copy-start | bytes 98308
  53.8 2.9 %copy-start.16 = (bf16[1,32,512]{2,1,0:T(8,128)(2,1)S(1)}, bf16[1,32,512]{2,1,0:T(8,128)(2,1)}, u32[]{:S(2)}) copy-start(bf16[1,32,512]{2,1,0:T(8,128)(2,1)} %param.9) | copy-start | bytes 98308
  53.8 2.9 %copy-start.18 = (bf16[32,512]{1,0:T(8,128)(2,1)S(1)}, bf16[32,512]{1,0:T(8,128)(2,1)}, u32[]{:S(2)}) copy-start(bf16[32,512]{1,0:T(8,128)(2,1)} %copy-done.17) | copy-start | bytes 98308
  53.8 2.9 %copy-start.22 = (bf16[32,512]{1,0:T(8,128)(2,1)S(1)}, bf16[32,512]{1,0:T(8,128)(2,1)}, u32[]{:S(2)}) copy-start(bf16[32,512]{1,0:T(8,128)(2,1)} %copy-done.21) | copy-start | bytes 98308
  177.7 2.9 %copy-start.2 = (f32[3,256,512]{2,1,0:T(8,128)S(1)}, f32[3,256,512]{2,1,0:T(8,128)}, u32[]{:S(2)}) copy-start(f32[3,256,512]{2,1,0:T(8,128)} %get-tuple-element.7) | copy-start | bytes 4718596
  177.7 4.2 %copy-start = (bf16[64,30720]{1,0:T(8,128)(2,1)S(1)}, bf16[64,30720]{1,0:T(8,128)(2,1)}, u32[]{:S(2)}) copy-start(bf16[64,30720]{1,0:T(8,128)(2,1)} %get-tuple-element.8) | copy-start | bytes 11796484

commit v2 on v1

v2 whole, which is shorter than its diff:
```python
import functools

import jax
import jax.numpy as jnp
from jax import lax
from jax.experimental import pallas as pl
from jax.experimental.pallas import tpu as pltpu
from jax.sharding import PartitionSpec as P

MESH_ID = pl.DeviceIdType.MESH
BF = jnp.bfloat16
F32 = jnp.float32

VOCAB_CHUNK = 768
CHUNKS = 5
HALF_VOCAB = VOCAB_CHUNK * CHUNKS
WEIGHT_UNITS = 6
FINISH_BLOCK = 6144
UNIT_ORDER = tuple(('e', i) for i in range(CHUNKS)) + (('w', 5), ('w', 4), ('t', 0), ('w', 3), ('w', 2), ('w', 1), ('w', 0))
GROUPS = ((0, 1), (1, 1), (2, 1), (3, 1), (4, 1))
TOUCH_GROUP = len(GROUPS)
CHAIN_SLOTS = ('p0', 'p1', 'a0 p2', 'a1 p3', 'a2 p4', 'a3', '', '', '', 's0 a4 s1', '', '', 's2 s3', '', 'l0', 's4 l2', 'l1 p5 l4 p6 l3', 'a5', 'a6 h p7 p8 a7')
TAIL_SLOTS = ('h p9 p10 h h a8 p11 a9 s5 s7 h h s6', 'a11 a10 h h s9 s8 h', 'l6 l5 l7 h', 's11 s10 h h h', 'l8 l9 h', 'l10 h', 'l11')


def gelu_and_slope(pre):
    return jax.jvp(jax.nn.gelu, (pre,), (jnp.ones_like(pre),))


def comm_kernel(stages, layers, vocab, ids_ref, slot_ref, touched_ref, cot_ref, stored_ref, w_in, w_out, acc_in, acc_out, acc_emb,
                gin_ref, gout_ref, emb_ref, patch_ref, x_ref, h_ref, g_ref, dh_ref, slope, cot_buf, cot_rcv,
                sem_w, sem_cs, sem_cr,
                u_in, r0_in, r1_in, r2_in, u_out, r0_out, r1_out, r2_out, u_e, r0_e, r1_e, r2_e, u_t, r0_t, r1_t, r2_t,
                ag, agt, dxb, st_in, st_out, st_e,
                sem_st_in, sem_st_out, sem_st_e, sem_t, s0s, s0r, s1s, s1r, s2s, s2r,
                dxs, dxr, own_s, fwd_s, pt_s, col_r, pt_r):
    s = lax.axis_index('pp')
    d = lax.axis_index('dp')
    c = lax.rem(d, 2)
    x = lax.rem(d // 2, 2)
    y = d // 4
    core_peer = d + 1 - 2 * c
    x_peer = d + 2 - 4 * x
    y_peer = d + 4 - 8 * y
    last = stages - 1

    def send(src, dst, ss, rs, target):
        return pltpu.make_async_remote_copy(src_ref=src, dst_ref=dst, send_sem=ss, recv_sem=rs, device_id=target, device_id_type=MESH_ID)

    barrier = pltpu.get_barrier_semaphore()
    for peer in (core_peer, x_peer, y_peer):
        pl.semaphore_signal(barrier, inc=1, device_id=(s, peer), device_id_type=MESH_ID)
    for off in range(1, stages):
        pl.semaphore_signal(barrier, inc=1, device_id=(lax.rem(s + off, stages), d), device_id_type=MESH_ID)

    def in_copy(n):
        unit, yx = n // 4, lax.rem(n, 4)
        slot = lax.rem(n, 2)
        return pltpu.make_async_copy(acc_in.at[layers - 1 - unit, pl.ds(yx * 128, 128), :], st_in.at[slot], sem_st_in.at[slot])

    def out_copy(n):
        unit, yx = n // 4, lax.rem(n, 4)
        slot = lax.rem(n, 2)
        return pltpu.make_async_copy(acc_out.at[layers - 1 - unit, pl.ds(yx * 512, 512), :], st_out.at[slot], sem_st_out.at[slot])

    part_rows = HALF_VOCAB * 4
    chunk_rows = VOCAB_CHUNK * 4
    tail_rows = vocab * 4 - (part_rows * 2 * stages - chunk_rows)

    def emb_copy(n, act):
        k, half = n // 2, n % 2
        slot = n % 2
        start = pl.multiple_of(s * (2 * part_rows) + half * part_rows + k * chunk_rows, 8)

        def full():
            act(pltpu.make_async_copy(acc_emb.at[pl.ds(start, chunk_rows), :], st_e.at[slot], sem_st_e.at[slot]))

        if k == CHUNKS - 1 and half == 1:
            @pl.when(s == last)
            def _():
                act(pltpu.make_async_copy(acc_emb.at[pl.ds(vocab * 4 - tail_rows, tail_rows), :],
                                          st_e.at[slot, pl.ds(0, tail_rows), :], sem_st_e.at[slot]))

            @pl.when(s != last)
            def _():
                full()
        else:
            full()

    w_copies = []
    for layer in range(layers):
        for j, (w, u) in enumerate(((w_in, u_in), (w_out, u_out))):
            w_copies.append(pltpu.make_async_copy(w.at[layer], u.at[layer], sem_w.at[2 * layer + j]))
            w_copies[-1].start()
    for n in range(2):
        in_copy(jnp.int32(n)).start()
        out_copy(jnp.int32(n)).start()
        emb_copy(n, lambda cp: cp.start())

    rows = cot_ref.shape[0]

    def dx_send(k, z):
        return send(dxb.at[k], dxb.at[k], dxs.at[k, z], dxr.at[k], (z, d))

    def cot_send(k, target):
        return send(cot_buf.at[k], cot_rcv.at[k], sem_cs.at[k], sem_cr.at[k], (target, d))

    def weight_produce(unit):
        layer = unit // 2
        if unit % 2 == 0:
            def body(yx, carry):
                n = 4 * (layers - 1 - layer) + yx
                slot = lax.rem(n, 2)
                in_copy(n).wait()
                lhs = x_ref[layer, :, pl.ds(pl.multiple_of(yx * 128, 128), 128)]
                for col in range(4):
                    cs = slice(col * 512, (col + 1) * 512)
                    new = lax.dot_general(lhs, dh_ref[layer, :, cs], (((0,), (0,)), ((), ())), preferred_element_type=F32)
                    tot = (st_in[slot, :, cs] + new).astype(BF)
                    u_in[layer, yx // 2, lax.rem(yx, 2), 0, :, cs] = tot[:64]
                    u_in[layer, yx // 2, lax.rem(yx, 2), 1, :, cs] = tot[64:]

                @pl.when(n + 2 < 12)
                def _():
                    in_copy(n + 2).start()
                return carry
        else:
            def body(yx, carry):
                n = 4 * (layers - 1 - layer) + yx
                slot = lax.rem(n, 2)
                out_copy(n).wait()
                for part in range(4):
                    rows = pl.ds(part * 128, 128)
                    lhs = h_ref[layer, :, pl.ds(pl.multiple_of(yx * 512 + part * 128, 128), 128)]
                    new = lax.dot_general(lhs, g_ref[layer], (((0,), (0,)), ((), ())), preferred_element_type=F32)
                    tot = (st_out[slot, rows, :] + new).astype(BF)
                    u_out[layer, yx // 2, lax.rem(yx, 2), part // 2, pl.ds((part % 2) * 128, 128), :] = tot

                @pl.when(n + 2 < 12)
                def _():
                    out_copy(n + 2).start()
                return carry
        lax.fori_loop(0, 4, body, 0)

    def emb_produce(k):
        for half in range(2):
            n = 2 * k + half
            emb_copy(n, lambda cp: cp.wait())

            def body(q, carry):
                u_e[k, q // 2, lax.rem(q, 2), half] = st_e[n % 2, pl.ds(q, VOCAB_CHUNK, stride=4), :].astype(BF)
                return carry
            lax.fori_loop(0, 4, body, 0)
            if n + 2 < 2 * CHUNKS:
                emb_copy(n + 2, lambda cp: cp.start())

    def touched_produce():
        @pl.when(s > 0)
        def _():
            for step in range(stages):
                dx_send(step, 0).wait_recv()
        for half in range(2):
            hot = (slot_ref[half * 128:(half + 1) * 128, :] == ids_ref[...]).astype(F32).astype(BF)
            for q in range(4):
                new = jnp.dot(hot, dxb[:, q].reshape(128, 128), preferred_element_type=F32)
                u_t[q // 2, q % 2, half] = (touched_ref[pl.ds(half * 512 + q, 128, stride=4), :] + new).astype(BF)

    def unit_bufs(kind, i):
        if kind == 'e':
            return u_e.at[i], r0_e.at[i], r1_e.at[i], r2_e.at[i], VOCAB_CHUNK
        if kind == 't':
            return u_t, r0_t, r1_t, r2_t, 128
        if i % 2 == 0:
            return u_in.at[i // 2], r0_in.at[i // 2], r1_in.at[i // 2], r2_in.at[i // 2], 64
        return u_out.at[i // 2], r0_out.at[i // 2], r1_out.at[i // 2], r2_out.at[i // 2], 256

    def core_send(pos):
        u, r0, r1, r2, rows = unit_bufs(*UNIT_ORDER[pos])
        return send(u.at[:, :, 1 - c], r0, s0s.at[pos], s0r.at[pos], (s, core_peer))

    def first_send(pos):
        u, r0, r1, r2, rows = unit_bufs(*UNIT_ORDER[pos])
        if pos % 2 == 0:
            return send(u.at[:, 1 - x, c], r1, s1s.at[pos], s1r.at[pos], (s, x_peer))
        return send(u.at[1 - y, :, c], r1, s1s.at[pos], s1r.at[pos], (s, y_peer))

    def second_send(pos):
        u, r0, r1, r2, rows = unit_bufs(*UNIT_ORDER[pos])
        if pos % 2 == 0:
            return send(u.at[1 - y, x, c], r2, s2s.at[pos], s2r.at[pos], (s, y_peer))
        return send(u.at[y, 1 - x, c], r2, s2s.at[pos], s2r.at[pos], (s, x_peer))

    def stage_produce(pos):
        kind, i = UNIT_ORDER[pos]
        if kind == 'w':
            weight_produce(i)
        elif kind == 't':
            touched_produce()
        else:
            emb_produce(i)
        core_send(pos).start()

    def stage_add(pos):
        u, r0, r1, r2, rows = unit_bufs(*UNIT_ORDER[pos])
        core_send(pos).wait_recv()
        far = [(j, 1 - x) for j in range(2)] if pos % 2 == 0 else [(1 - y, j) for j in range(2)]
        near = [(j, x) for j in range(2)] if pos % 2 == 0 else [(y, j) for j in range(2)]
        for a, b in far:
            u[a, b, c] = u[a, b, c] + r0[a, b]
        first_send(pos).start()
        for a, b in near:
            u[a, b, c] = u[a, b, c] + r0[a, b]

    def stage_second(pos):
        u, r0, r1, r2, rows = unit_bufs(*UNIT_ORDER[pos])
        first_send(pos).wait_recv()
        far, i = ((1 - y, x), 1 - y) if pos % 2 == 0 else ((y, 1 - x), 1 - x)
        u[far[0], far[1], c] = u[far[0], far[1], c] + r1[i]
        second_send(pos).start()
        u[y, x, c] = u[y, x, c] + r1[1 - i]

    def piece(p, k):
        return agt.at[p] if k == TOUCH_GROUP else ag.at[p, pl.ds(*GROUPS[k])]

    def own_sends(k, act):
        for j, off in enumerate((1, -1) if k != TOUCH_GROUP else (1, -1, 2, -2, 3, -3)):
            @pl.when((s + off >= 0) & (s + off <= last))
            def _():
                blk = piece(2 * s + c, k)
                act(send(blk, blk, own_s.at[j, k], col_r.at[s, k], (jnp.clip(s + off, 0, last), d)))

    def far_send(k, hop, sign, act):
        z = s - sign * hop

        @pl.when((z >= 0) & (z <= last) & (s + sign >= 0) & (s + sign <= last))
        def _():
            zc = jnp.clip(z, 0, last)
            blk = piece(2 * zc + c, k)
            act(send(blk, blk, fwd_s.at[zc, k], col_r.at[zc, k], (jnp.clip(s + sign, 0, last), d)))

    def col_wait(z, k):
        blk = piece(2 * z + c, k)
        send(blk, blk, fwd_s.at[0, 0], col_r.at[z, k], (s, d)).wait_recv()

    def part_send(z, k):
        blk = piece(2 * z + c, k)
        return send(blk, blk, pt_s.at[z, k], pt_r.at[z, k], (s, core_peer))

    def emb_write(p, k):
        dst = patch_ref.at[p] if k == TOUCH_GROUP else emb_ref.at[p, pl.ds(*GROUPS[k])]
        return pltpu.make_async_copy(piece(p, k), dst, sem_t.at[p, k])

    def emit(p, k):
        emb_write(p, k).start()

    def have_piece(z, k):
        part_send(z, k).start()
        emit(2 * z + c, k)

    def stage_last(pos):
        kind, i = UNIT_ORDER[pos]
        u, r0, r1, r2, rows = unit_bufs(kind, i)
        second_send(pos).wait_recv()
        if kind == 'e':
            ag[2 * s + c, i] = u[y, x, c] + r2[...]
            for k, (first, count) in enumerate(GROUPS):
                if i == first + count - 1:
                    own_sends(k, lambda cp: cp.start())
                    have_piece(s, k)
        elif kind == 't':
            agt[2 * s + c] = u[y, x, c] + r2[...]
            own_sends(TOUCH_GROUP, lambda cp: cp.start())
            have_piece(s, TOUCH_GROUP)
        else:
            tot = (u[y, x, c].astype(F32) + r2[...].astype(F32))
            if i % 2 == 0:
                gin_ref[i // 2] = tot
            else:
                gout_ref[i // 2] = tot

    def part_event(z, k):
        part_send(z, k).wait_recv()
        emit(2 * z + 1 - c, k)

    def hop_event(k, hop):
        for sign in (-1, 1):
            z = s - sign * hop

            @pl.when((z >= 0) & (z <= last))
            def _():
                col_wait(jnp.clip(z, 0, last), k)
            if k != TOUCH_GROUP:
                far_send(k, hop, sign, lambda cp: cp.start())

            @pl.when((z >= 0) & (z <= last))
            def _():
                have_piece(jnp.clip(z, 0, last), k)

    events = [(k, hop) for hop in (1, 2, 3) for k in (0, 2, 1, 4, 3)]

    def run(slot):
        for op in slot.split():
            if op == 'h':
                hop_event(*events.pop(0))
            else:
                {'p': stage_produce, 'a': stage_add, 's': stage_second, 'l': stage_last}[op[0]](int(op[1:]))

    for k in range(stages):
        x_ref[0, k * rows:(k + 1) * rows, :] = stored_ref[jnp.maximum(last - s - k, 0)]
    pl.semaphore_wait(barrier, 3 + stages - 1)
    slots = list(CHAIN_SLOTS)
    run(slots.pop(0))
    for layer in range(layers):
        w_copies[2 * layer].wait()
        x_cur = x_ref[layer]
        for i in range(4):
            cs = slice(i * 512, (i + 1) * 512)
            pre = jnp.dot(x_cur, u_in[layer, :, :, :, :, cs].reshape(512, 512), preferred_element_type=F32).astype(BF)
            act, der = gelu_and_slope(pre.astype(F32))
            h_ref[layer, :, cs] = act.astype(BF)
            slope[layer, :, cs] = der
        run(slots.pop(0))
        w_copies[2 * layer + 1].wait()
        if layer < layers - 1:
            out = jnp.dot(h_ref[layer], u_out[layer].reshape(2048, 512), preferred_element_type=F32)
            x_ref[layer + 1] = (x_cur.astype(F32) + out).astype(BF)
        run(slots.pop(0))

    for k in range(stages):
        rs = slice(k * rows, (k + 1) * rows)
        active = s + k <= last
        for layer in range(layers - 1, -1, -1):
            @pl.when(active)
            def _():
                if layer < layers - 1:
                    cot = g_ref[layer, rs, :]
                else:
                    if k > 0:
                        cot_send(k - 1, s).wait_recv()
                        cot = cot_rcv[k - 1]
                    else:
                        cot = cot_ref[...]
                    g_ref[layer, rs, :] = cot
                back = cot.astype(F32)
                for i in range(4):
                    cs = slice(i * 512, (i + 1) * 512)
                    dh = lax.dot_general(cot, u_out[layer, i // 2, i % 2].reshape(512, 512), (((1,), (1,)), ((), ())), preferred_element_type=F32).astype(BF)
                    dh = (dh.astype(F32) * slope[layer, rs, cs]).astype(BF)
                    dh_ref[layer, rs, cs] = dh
                    back = back + lax.dot_general(dh, u_in[layer, :, :, :, :, cs].reshape(512, 512), (((1,), (1,)), ((), ())), preferred_element_type=F32)
                cot = back.astype(BF)
                if layer > 0:
                    g_ref[layer - 1, rs, :] = cot
                else:
                    cot_buf[k] = cot

                    @pl.when(s > 0)
                    def _():
                        cot_send(k, jnp.maximum(s - 1, 0)).start()

                    @pl.when(s == 0)
                    def _():
                        for q in range(4):
                            dxb[k, q] = cot[:, q * 128:(q + 1) * 128]
                        for z in range(1, stages):
                            dx_send(k, z).start()

            @pl.when(jnp.logical_not(active))
            def _():
                g_ref[layer, rs, :] = jnp.zeros((rows, 512), BF)
                dh_ref[layer, rs, :] = jnp.zeros((rows, 2048), BF)
            run(slots.pop(0))

    total = len(UNIT_ORDER)
    for slot in TAIL_SLOTS:
        run(slot)
    for hop in (1, 2, 3):
        hop_event(TOUCH_GROUP, hop)

    for k in range(TOUCH_GROUP + 1):
        for z in range(stages):
            part_event(z, k)

    for pos in range(total):
        core_send(pos).wait_send()
        first_send(pos).wait_send()
        second_send(pos).wait_send()

    for k in range(stages):
        @pl.when(s == 0)
        def _():
            for z in range(1, stages):
                dx_send(k, z).wait_send()

        @pl.when((s > 0) & (s + k <= last))
        def _():
            cot_send(k, jnp.maximum(s - 1, 0)).wait_send()

    def drain(z, k):
        part_send(z, k).wait_send()
        for core in range(2):
            emb_write(2 * z + core, k).wait()

    for k in range(TOUCH_GROUP + 1):
        for z in range(stages):
            drain(z, k)
    for k in range(TOUCH_GROUP + 1):
        own_sends(k, lambda cp: cp.wait_send())
        if k != TOUCH_GROUP:
            for hop in (1, 2):
                for sign in (-1, 1):
                    far_send(k, hop, sign, lambda cp: cp.wait_send())


def share_kernel(replicas, own_ref, all_ref, buf, send_sem, recv_sem):
    s = lax.axis_index('pp')
    d = lax.axis_index('dp')
    barrier = pltpu.get_barrier_semaphore()
    for off in range(1, replicas):
        pl.semaphore_signal(barrier, inc=1, device_id=(s, lax.rem(d + off, replicas)), device_id_type=MESH_ID)
    pl.semaphore_wait(barrier, replicas - 1)

    def copy(off):
        return pltpu.make_async_remote_copy(src_ref=own_ref, dst_ref=buf.at[d], send_sem=send_sem.at[off], recv_sem=recv_sem.at[d],
                                            device_id=(s, lax.rem(d + off, replicas)), device_id_type=MESH_ID)
    for off in range(1, replicas):
        copy(off).start()
    buf[d] = own_ref[...]
    for off in range(1, replicas):
        src = lax.rem(d + off, replicas)
        pltpu.make_async_remote_copy(src_ref=own_ref, dst_ref=buf.at[src], send_sem=send_sem.at[off], recv_sem=recv_sem.at[src],
                                     device_id=(s, src), device_id_type=MESH_ID).wait_recv()
    for off in range(1, replicas):
        copy(off).wait_send()
    all_ref[...] = buf[...]


def gather_kernel(ids_ref, emb_ref, out_ref, sem):
    replicas, _, tokens = ids_ref.shape
    z = lax.axis_index('pp')

    def body(i, carry):
        r, t = i // (tokens // 8), lax.rem(i, tokens // 8) * 8
        for j in range(8):
            pltpu.make_async_copy(emb_ref.at[ids_ref[r, z, t + j]], out_ref.at[i * 8 + j], sem).start()
        return carry
    lax.fori_loop(0, replicas * tokens // 8, body, 0)
    pltpu.make_async_copy(emb_ref.at[pl.ds(0, replicas * tokens)], out_ref, sem).wait()


def finish_kernel(scale, ids_ref, base_ref, patch_ref, gin_ref, gout_ref, emb_out, gin_out, gout_out, rows_f, patch_f, stage, sem):
    step = pl.program_id(0)
    core = lax.rem(lax.axis_index('dp'), 2)
    chunks = base_ref.shape[0]

    @pl.when(step == 0)
    def _():
        def copy(i):
            return pltpu.make_async_copy(base_ref.at[i], stage.at[i], sem.at[i])
        for i in range(chunks):
            copy(i).start()
        gin_out[...] = gin_ref[...] * scale
        gout_out[...] = gout_ref[...] * scale
        patch_f[...] = patch_ref[...].astype(F32)

        def widen(i, carry):
            copy(i).wait()
            rows_f[pl.ds(pl.multiple_of(i * VOCAB_CHUNK, VOCAB_CHUNK), VOCAB_CHUNK), :] = stage[i].astype(F32)
            return carry
        lax.fori_loop(0, chunks, widen, 0)

        replicas, stages, tokens = ids_ref.shape

        def put(i, carry):
            z, r, t = i // (replicas * tokens // 8), lax.rem(i // (tokens // 8), replicas), lax.rem(i, tokens // 8) * 8
            for j in range(8):
                rows_f[pl.ds(ids_ref[r, z, t + j], 1), :] = patch_f[pl.ds(i * 8 + j, 1), :]
            return carry
        lax.fori_loop(0, patch_f.shape[0] // 8, put, 0)

    pick = lax.broadcasted_iota(jnp.int32, (64, 128), 1) == lax.broadcasted_iota(jnp.int32, (64, 128), 0) + 64 * core
    sel = jnp.where(pick, scale, 0.0).astype(BF)
    for i in range(FINISH_BLOCK // VOCAB_CHUNK):
        start = pl.multiple_of(step * FINISH_BLOCK + i * VOCAB_CHUNK, VOCAB_CHUNK)
        block = rows_f[pl.ds(start, VOCAB_CHUNK), :].astype(BF)
        emb_out[:, i * VOCAB_CHUNK:(i + 1) * VOCAB_CHUNK] = lax.dot_general(sel, block, (((1,), (1,)), ((), ())), preferred_element_type=F32)


def solution(mesh):
    stages = mesh.shape['pp']
    replicas = mesh.shape['dp']

    def device_body(tok_ids, d_out, stored_x, w_in, w_out, acc_in, acc_out, acc_emb):
        layers, hid, ff = w_in.shape
        vocab = acc_emb.shape[1]
        tokens = d_out.shape[1]
        rows = tokens * stages
        steps_ids = tok_ids[::-1]
        ids = steps_ids.reshape(1, rows)
        vm = pl.BlockSpec(memory_space=pltpu.VMEM)
        hbm = pl.BlockSpec(memory_space=pltpu.HBM)
        smem = pl.BlockSpec(memory_space=pltpu.SMEM)
        dma = pltpu.SemaphoreType.DMA
        slot_ids = pl.pallas_call(
            functools.partial(share_kernel, replicas),
            out_shape=jax.ShapeDtypeStruct((replicas, stages, tokens), jnp.int32),
            in_specs=[vm], out_specs=vm,
            scratch_shapes=[pltpu.VMEM((replicas, stages, tokens), jnp.int32), dma((replicas,)), dma((replicas,))],
            compiler_params=pltpu.CompilerParams(collective_id=1, has_side_effects=True),
            name='share_ids',
        )(steps_ids)
        own_slots = lax.dynamic_index_in_dim(slot_ids, lax.axis_index('pp'), axis=1, keepdims=False)
        touched = pl.pallas_call(
            gather_kernel,
            out_shape=jax.ShapeDtypeStruct((replicas * tokens, 4, 128), F32),
            in_specs=[smem, hbm], out_specs=vm, scratch_shapes=[pltpu.SemaphoreType.DMA],
            name='gather_rows',
        )(slot_ids, acc_emb.reshape(vocab, 4, 128))
        v = pltpu.VMEM
        dma = pltpu.SemaphoreType.DMA
        units = len(UNIT_ORDER)
        gin, gout, emb, patch = pl.pallas_call(
            functools.partial(comm_kernel, stages, layers, vocab),
            out_shape=(jax.ShapeDtypeStruct((layers, hid // 8, ff), F32), jax.ShapeDtypeStruct((layers, ff // 8, hid), F32),
                       jax.ShapeDtypeStruct((2 * stages, CHUNKS, VOCAB_CHUNK, 128), BF), jax.ShapeDtypeStruct((2 * stages, 128, 128), BF)),
            in_specs=[vm] * 5 + [hbm] * 5,
            out_specs=(vm, vm, hbm, hbm),
            scratch_shapes=[
                v((layers, rows, hid), BF), v((layers, rows, ff), BF), v((layers, rows, hid), BF), v((layers, rows, ff), BF), v((layers, rows, ff), F32),
                v((stages, tokens, hid), BF), v((stages, tokens, hid), BF), dma((2 * layers,)), dma((stages,)), dma((stages,)),
                v((layers, 2, 2, 2, 64, ff), BF), v((layers, 2, 2, 64, ff), BF), v((layers, 2, 64, ff), BF), v((layers, 64, ff), BF),
                v((layers, 2, 2, 2, 256, hid), BF), v((layers, 2, 2, 256, hid), BF), v((layers, 2, 256, hid), BF), v((layers, 256, hid), BF),
                v((CHUNKS, 2, 2, 2, VOCAB_CHUNK, 128), BF), v((CHUNKS, 2, 2, VOCAB_CHUNK, 128), BF), v((CHUNKS, 2, VOCAB_CHUNK, 128), BF), v((CHUNKS, VOCAB_CHUNK, 128), BF),
                v((2, 2, 2, 128, 128), BF), v((2, 2, 128, 128), BF), v((2, 128, 128), BF), v((128, 128), BF),
                v((2 * stages, CHUNKS, VOCAB_CHUNK, 128), BF), v((2 * stages, 128, 128), BF), v((stages, 4, tokens, 128), BF),
                v((2, 128, ff), F32), v((2, 512, hid), F32), v((2, VOCAB_CHUNK * 4, 128), F32),
                dma((2,)), dma((2,)), dma((2,)), dma((2 * stages, CHUNKS + 1)),
                dma((units,)), dma((units,)), dma((units,)), dma((units,)), dma((units,)), dma((units,)),
                dma((stages, stages)), dma((stages,)), dma((6, CHUNKS + 1)), dma((stages, CHUNKS)), dma((stages, CHUNKS + 1)), dma((stages, CHUNKS + 1)), dma((stages, CHUNKS + 1)),
            ],
            compiler_params=pltpu.CompilerParams(collective_id=0, has_side_effects=True, vmem_limit_bytes=67043328),
            name='reduce_exchange',
        )(ids, own_slots.reshape(-1, 1), touched.reshape(-1, 128), d_out[0], stored_x[0], w_in.reshape(layers, 2, 2, 2, 64, ff), w_out.reshape(layers, 2, 2, 2, 256, hid), acc_in.reshape(layers, hid, ff), acc_out.reshape(layers, ff, hid), acc_emb.reshape(vocab * 4, 128))
        grad_emb, grad_in, grad_out = pl.pallas_call(
            functools.partial(finish_kernel, 1.0 / replicas),
            out_shape=(jax.ShapeDtypeStruct((64, vocab), F32), jax.ShapeDtypeStruct(gin.shape, F32), jax.ShapeDtypeStruct(gout.shape, F32)),
            grid=(2 * stages * HALF_VOCAB // FINISH_BLOCK,),
            in_specs=[smem, hbm, vm, vm, vm],
            out_specs=(pl.BlockSpec((64, FINISH_BLOCK), lambda i: (0, i)), vm, vm),
            scratch_shapes=[v((2 * stages * CHUNKS * VOCAB_CHUNK, 128), F32), v((stages * replicas * tokens, 128), F32),
                            v((2 * stages * CHUNKS, VOCAB_CHUNK, 128), BF), dma((2 * stages * CHUNKS,))],
            compiler_params=pltpu.CompilerParams(vmem_limit_bytes=58 * 2 ** 20, dimension_semantics=('arbitrary',)),
            name='finish',
        )(slot_ids, emb.reshape(2 * stages * CHUNKS, VOCAB_CHUNK, 128), patch.reshape(-1, 128), gin, gout)
        return grad_in, grad_out, grad_emb.T

    return jax.shard_map(device_body, mesh=mesh, in_specs=(P(None, 'dp'), P('pp', 'dp', None), P('pp', None, 'dp', None), P('pp', None, None), P('pp', None, None), P('pp', 'dp', None, None), P('pp', 'dp', None, None), P('dp', None, None)), out_specs=(P('pp', 'dp', None), P('pp', 'dp', None), P(None, 'dp')), check_vma=False)
```

time: 188 us -> 149 us (0.79)
  matrix products: 35.2 us -> 0 us
  Pallas kernels: 119 us -> 145 us
  other arithmetic: 15.1 us -> 0 us
  starting transfers between devices: 9.66 us -> 0 us
    dot_general x29 -> x0, matrix products: 35.2 us -> none  [the longest x12 14.1 us: chain_xla(): lax.dot_general(d_pre, w_in[layer_id], (((1,), (1,)), ((), ())), preferre...]
    pallas_call x1 -> x4, Pallas kernels: 119 us -> 145 us  [the longest x1 118 us: device_body(): pl.pallas_call(functools.partial(comm_kernel, stages, layers, vocab), out...]
    ppermute x3 -> x0, starting transfers between devices: 9.66 us -> none  [chain_xla(): lax.ppermute(cot, 'pp', [(sender, sender - 1) for sender in range(1, stag...]
    another operation x12 -> x0, other arithmetic: 5.77 us -> none  [the longest x2 1.95 us: chain_xla(): hs = jnp.stack([s[1] for s in saved])]
    transpose x2 -> x0, other arithmetic: 5.19 us -> none  [the longest x1 3.72 us: device_body(): grad_emb = (emb[:, :vocab].astype(F32) * scale).T]
    mul x2 -> x0, other arithmetic: 4.19 us -> none  [device_body(): return (gin * scale, gout * scale, grad_emb)]
    unnamed x80 -> x2, local copies, waits for them, and re-layouts: 2.23 us -> 0.01 us
  transfers between devices with their start and end apart: 3 -> 0, of which waited for: 1 -> 0; matrix products, arithmetic and copies ran while one was open for 1% -> 0% of each run, Pallas kernels for 0% -> 0%
where the time goes in v2:
time: 149 us; the launch traced here: 148 us
  Pallas kernels  145 us (97%)
  local copies, waits for them, and re-layouts  2.83 us (2%)
    pallas_call x1, Pallas kernels, device_body(): pl.pallas_call(functools.partial(comm_kernel, stages, layers, vocab), out...  118 us
    pallas_call x1, Pallas kernels, device_body(): pl.pallas_call(functools.partial(finish_kernel, 1.0 / replicas), out_shap...  16.2 us
    pallas_call x1, Pallas kernels, device_body(): pl.pallas_call(functools.partial(share_kernel, replicas), out_shape=jax.S...  6.34 us
    pallas_call x1, Pallas kernels, device_body(): pl.pallas_call(gather_kernel, out_shape=jax.ShapeDtypeStruct((replicas *...  3.66 us

profile of v2, /device:TPU:25, one launch (start us, length us, event | category | flops | bytes accessed | tf_op | source)
XLA Modules:
  0.0 148.4 jit_solution(10443241949316815804)
XLA Ops:
  0.6 0.7 rev.3.own_ref
  1.3 0.0 copy-start
  1.3 0.6 reshape.40.ids_ref
  1.9 0.0 copy-done
  1.9 6.3 %share_ids.1.ids_ref = s32[8,4,32]{2,1,0:T(4,128)} custom-call(s32[4,32]{1,0:T(4,128)} %copy-done), custom_call_target="tpu_custom_call" | custom-call | tf_op jit(solution)/shard_map/share_ids/pallas_call | solution.py:504
  8.3 0.7 dynamic-slice_reduce_fusion
  9.0 0.8 reshape.51.slot_ref
  9.8 3.7 %gather_rows.1 = f32[256,4,128]{2,1,0:T(4,128)} custom-call(s32[8,4,32]{2,1,0:T(4,128)} %share_ids.1.ids_ref, f32[30522,4,128]{2,1,0:T(4,128)} %bitcast.12), custom_call_target="tpu_custom_call" | custom-call | tf_op jit(solution)/shard_map/gather_rows/pallas_call | solution.py:513
  13.5 118.5 %reduce_exchange.1 = (f32[3,64,2048]{2,1,0:T(8,128)}, f32[3,256,512]{2,1,0:T(8,128)}, bf16[8,5,768,128]{3,2,1,0:T(8,128)(2,1)}, bf16[8,128,128]{2,1,0:T(8,128)(2,1)}) custom-call(s32[1,128]{1,0:T(1,128)} %reshape.40.ids_ref, s32[256,1]{1,0:T(8,128)} %reshape.51.slot_ref, f32[1024,128]{1,0:T(8,128)} %bitcast.19, bf16[32,512]{1,0:T(8,128)(2,1)} %bitcast.22, ...), custom_call_target="tpu_custom_call" | custom-call | tf_op jit(solution)/shard_map/reduce_exchange/pallas_call | solution.py:522
  132.0 16.2 %finish.1 = (f32[64,30522]{1,0:T(8,128)}, f32[3,64,2048]{2,1,0:T(8,128)}, f32[3,256,512]{2,1,0:T(8,128)}) custom-call(s32[8,4,32]{2,1,0:T(4,128)} %share_ids.1.ids_ref, bf16[40,768,128]{2,1,0:T(8,128)(2,1)} %bitcast.16, bf16[1024,128]{1,0:T(8,128)(2,1)} %bitcast.20, f32[3,64,2048]{2,1,0:T(8,128)} %get-tuple-element.12.gin_ref, ...), custom_call_target="tpu_custom_call" | custom-call | tf_op jit(solution)/shard_map/finish/pallas_call | solution.py:544
Async XLA Ops:
  1.3 0.6 copy-start

commit v3 on v2

--- a/solution.py
+++ b/solution.py
@@ -15,12 +15,40 @@
 CHUNKS = 5
 HALF_VOCAB = VOCAB_CHUNK * CHUNKS
 WEIGHT_UNITS = 6
-FINISH_BLOCK = 6144
+FINISH_BLOCK = 3072
 UNIT_ORDER = tuple(('e', i) for i in range(CHUNKS)) + (('w', 5), ('w', 4), ('t', 0), ('w', 3), ('w', 2), ('w', 1), ('w', 0))
 GROUPS = ((0, 1), (1, 1), (2, 1), (3, 1), (4, 1))
 TOUCH_GROUP = len(GROUPS)
-CHAIN_SLOTS = ('p0', 'p1', 'a0 p2', 'a1 p3', 'a2 p4', 'a3', '', '', '', 's0 a4 s1', '', '', 's2 s3', '', 'l0', 's4 l2', 'l1 p5 l4 p6 l3', 'a5', 'a6 h p7 p8 a7')
-TAIL_SLOTS = ('h p9 p10 h h a8 p11 a9 s5 s7 h h s6', 'a11 a10 h h s9 s8 h', 'l6 l5 l7 h', 's11 s10 h h h', 'l8 l9 h', 'l10 h', 'l11')
+CHAIN_SLOTS = (
+    ('p0',),
+    ('p1',),
+    ('a0', 'p2'),
+    ('a1', 'p3'),
+    ('a2', 'p4'),
+    (),
+    (),
+    (),
+    (),
+    ('s0', 'a3', 's1', 'a4'),
+    (),
+    (),
+    ('l0', 's2'),
+    ('l1',),
+    (),
+    ('s3', 'h'),
+    ('s4', 'l2', 'p5', 'h', 'p6'),
+    ('a5', 'l3'),
+    ('a6', 'l4', 'h', 'p7', 'p8', 'a7'),
+)
+TAIL_SLOTS = (
+    ('p9', 'p10', 'h', 'a8', 'p11', 'h', 'a9', 's5', 's7', 'h', 's6'),
+    ('a11', 'a10', 'h', 'h', 's9', 's8', 'h'),
+    ('l6', 'l5', 'l7', 'h'),
+    ('s11', 's10', 'h', 'h', 'h'),
+    ('l8', 'l9', 'h'),
+    ('l10', 'h'),
+    ('l11',),
+)
 
 
 def gelu_and_slope(pre):
@@ -159,11 +187,12 @@
         def _():
             for step in range(stages):
                 dx_send(step, 0).wait_recv()
-        for half in range(2):
-            hot = (slot_ref[half * 128:(half + 1) * 128, :] == ids_ref[...]).astype(F32).astype(BF)
+        for r in range(8):
+            hot = (ids_ref[...] == slot_ref[r, pl.ds(last - s, 1), :]).astype(F32).astype(BF)
             for q in range(4):
-                new = jnp.dot(hot, dxb[:, q].reshape(128, 128), preferred_element_type=F32)
-                u_t[q // 2, q % 2, half] = (touched_ref[pl.ds(half * 512 + q, 128, stride=4), :] + new).astype(BF)
+                new = lax.dot_general(hot, dxb[:, q].reshape(128, 128), (((0,), (0,)), ((), ())), preferred_element_type=F32)
+                old = touched_ref[pl.ds(r * 128 + q, 32, stride=4), :]
+                u_t[q // 2, q % 2, r // 4, (r % 4) * 32:(r % 4 + 1) * 32, :] = (old + new).astype(BF)
 
     def unit_bufs(kind, i):
         if kind == 'e':
@@ -296,10 +325,10 @@
             def _():
                 have_piece(jnp.clip(z, 0, last), k)
 
-    events = [(k, hop) for hop in (1, 2, 3) for k in (0, 2, 1, 4, 3)]
+    events = [(k, hop) for hop in (1, 2, 3) for k in range(TOUCH_GROUP)]
 
     def run(slot):
-        for op in slot.split():
+        for op in slot:
             if op == 'h':
                 hop_event(*events.pop(0))
             else:
@@ -437,7 +466,7 @@
 
 def gather_kernel(ids_ref, emb_ref, out_ref, sem):
     replicas, _, tokens = ids_ref.shape
-    z = lax.axis_index('pp')
+    z = ids_ref.shape[1] - 1 - lax.axis_index('pp')
 
     def body(i, carry):
         r, t = i // (tokens // 8), lax.rem(i, tokens // 8) * 8
@@ -456,7 +485,7 @@
     @pl.when(step == 0)
     def _():
         def copy(i):
-            return pltpu.make_async_copy(base_ref.at[i], stage.at[i], sem.at[i])
+            return pltpu.make_async_copy(base_ref.at[i], stage.at[pl.ds(pl.multiple_of(i * VOCAB_CHUNK, VOCAB_CHUNK), VOCAB_CHUNK), :], sem.at[i])
         for i in range(chunks):
             copy(i).start()
         gin_out[...] = gin_ref[...] * scale
@@ -465,7 +494,8 @@
 
         def widen(i, carry):
             copy(i).wait()
-            rows_f[pl.ds(pl.multiple_of(i * VOCAB_CHUNK, VOCAB_CHUNK), VOCAB_CHUNK), :] = stage[i].astype(F32)
+            chunk = pl.ds(pl.multiple_of(i * VOCAB_CHUNK, VOCAB_CHUNK), VOCAB_CHUNK)
+            rows_f[chunk, :] = stage[chunk, :].astype(F32)
             return carry
         lax.fori_loop(0, chunks, widen, 0)
 
@@ -474,7 +504,7 @@
         def put(i, carry):
             z, r, t = i // (replicas * tokens // 8), lax.rem(i // (tokens // 8), replicas), lax.rem(i, tokens // 8) * 8
             for j in range(8):
-                rows_f[pl.ds(ids_ref[r, z, t + j], 1), :] = patch_f[pl.ds(i * 8 + j, 1), :]
+                rows_f[pl.ds(ids_ref[r, stages - 1 - z, t + j], 1), :] = patch_f[pl.ds(i * 8 + j, 1), :]
             return carry
         lax.fori_loop(0, patch_f.shape[0] // 8, put, 0)
 
@@ -495,8 +525,7 @@
         vocab = acc_emb.shape[1]
         tokens = d_out.shape[1]
         rows = tokens * stages
-        steps_ids = tok_ids[::-1]
-        ids = steps_ids.reshape(1, rows)
+        ids = tok_ids[::-1].reshape(rows, 1)
         vm = pl.BlockSpec(memory_space=pltpu.VMEM)
         hbm = pl.BlockSpec(memory_space=pltpu.HBM)
         smem = pl.BlockSpec(memory_space=pltpu.SMEM)
@@ -508,8 +537,7 @@
             scratch_shapes=[pltpu.VMEM((replicas, stages, tokens), jnp.int32), dma((replicas,)), dma((replicas,))],
             compiler_params=pltpu.CompilerParams(collective_id=1, has_side_effects=True),
             name='share_ids',
-        )(steps_ids)
-        own_slots = lax.dynamic_index_in_dim(slot_ids, lax.axis_index('pp'), axis=1, keepdims=False)
+        )(tok_ids)
         touched = pl.pallas_call(
             gather_kernel,
             out_shape=jax.ShapeDtypeStruct((replicas * tokens, 4, 128), F32),
@@ -540,7 +568,7 @@
             ],
             compiler_params=pltpu.CompilerParams(collective_id=0, has_side_effects=True, vmem_limit_bytes=67043328),
             name='reduce_exchange',
-        )(ids, own_slots.reshape(-1, 1), touched.reshape(-1, 128), d_out[0], stored_x[0], w_in.reshape(layers, 2, 2, 2, 64, ff), w_out.reshape(layers, 2, 2, 2, 256, hid), acc_in.reshape(layers, hid, ff), acc_out.reshape(layers, ff, hid), acc_emb.reshape(vocab * 4, 128))
+        )(ids, slot_ids, touched.reshape(-1, 128), d_out[0], stored_x[0], w_in.reshape(layers, 2, 2, 2, 64, ff), w_out.reshape(layers, 2, 2, 2, 256, hid), acc_in.reshape(layers, hid, ff), acc_out.reshape(layers, ff, hid), acc_emb.reshape(vocab * 4, 128))
         grad_emb, grad_in, grad_out = pl.pallas_call(
             functools.partial(finish_kernel, 1.0 / replicas),
             out_shape=(jax.ShapeDtypeStruct((64, vocab), F32), jax.ShapeDtypeStruct(gin.shape, F32), jax.ShapeDtypeStruct(gout.shape, F32)),
@@ -548,7 +576,7 @@
             in_specs=[smem, hbm, vm, vm, vm],
             out_specs=(pl.BlockSpec((64, FINISH_BLOCK), lambda i: (0, i)), vm, vm),
             scratch_shapes=[v((2 * stages * CHUNKS * VOCAB_CHUNK, 128), F32), v((stages * replicas * tokens, 128), F32),
-                            v((2 * stages * CHUNKS, VOCAB_CHUNK, 128), BF), dma((2 * stages * CHUNKS,))],
+                            v((2 * stages * CHUNKS * VOCAB_CHUNK, 128), BF), dma((2 * stages * CHUNKS,))],
             compiler_params=pltpu.CompilerParams(vmem_limit_bytes=58 * 2 ** 20, dimension_semantics=('arbitrary',)),
             name='finish',
         )(slot_ids, emb.reshape(2 * stages * CHUNKS, VOCAB_CHUNK, 128), patch.reshape(-1, 128), gin, gout)

time: 149 us -> 146 us (0.980)
  Pallas kernels: 145 us -> 143 us
    pallas_call x1, Pallas kernels: 118 us -> 115 us  [device_body(): pl.pallas_call(functools.partial(comm_kernel, stages, layers, vocab), out...]
    pallas_call x1, Pallas kernels: 16.2 us -> 17.7 us  [device_body(): pl.pallas_call(functools.partial(finish_kernel, 1.0 / replicas), out_shap...]
where the time goes in v3:
time: 146 us; the launch traced here: 145 us
  Pallas kernels  143 us (98%)
    pallas_call x1, Pallas kernels, device_body(): pl.pallas_call(functools.partial(comm_kernel, stages, layers, vocab), out...  115 us
    pallas_call x1, Pallas kernels, device_body(): pl.pallas_call(functools.partial(finish_kernel, 1.0 / replicas), out_shap...  17.7 us
    pallas_call x1, Pallas kernels, device_body(): pl.pallas_call(functools.partial(share_kernel, replicas), out_shape=jax.S...  6.34 us
    pallas_call x1, Pallas kernels, device_body(): pl.pallas_call(gather_kernel, out_shape=jax.ShapeDtypeStruct((replicas *...  3.66 us

profile of v3, /device:TPU:25, one launch (start us, length us, event | category | flops | bytes accessed | tf_op | source)
XLA Modules:
  0.0 145.2 jit_solution(13610498247959278593)
XLA Ops:
  0.6 0.7 rev.3
  1.3 6.3 %share_ids.1.ids_ref.slot_ref = s32[8,4,32]{2,1,0:T(4,128)} custom-call(s32[4,32]{1,0:T(4,128)} %own_ref.1), custom_call_target="tpu_custom_call" | custom-call | tf_op jit(solution)/shard_map/share_ids/pallas_call | solution.py:533
  7.7 0.7 reshape.46.ids_ref
  8.4 3.7 %gather_rows.1 = f32[256,4,128]{2,1,0:T(4,128)} custom-call(s32[8,4,32]{2,1,0:T(4,128)} %share_ids.1.ids_ref.slot_ref, f32[30522,4,128]{2,1,0:T(4,128)} %bitcast.12), custom_call_target="tpu_custom_call" | custom-call | tf_op jit(solution)/shard_map/gather_rows/pallas_call | solution.py:541
  12.1 115.2 %reduce_exchange.1 = (f32[3,64,2048]{2,1,0:T(8,128)}, f32[3,256,512]{2,1,0:T(8,128)}, bf16[8,5,768,128]{3,2,1,0:T(8,128)(2,1)}, bf16[8,128,128]{2,1,0:T(8,128)(2,1)}) custom-call(s32[128,1]{1,0:T(8,128)} %reshape.46.ids_ref, s32[8,4,32]{2,1,0:T(4,128)} %share_ids.1.ids_ref.slot_ref, f32[1024,128]{1,0:T(8,128)} %bitcast.19, bf16[32,512]{1,0:T(8,128)(2,1)} %bitcast.22, ...), custom_call_target="tpu_custom_call" | custom-call | tf_op jit(solution)/shard_map/reduce_exchange/pallas_call | solution.py:550
  127.3 17.7 %finish.1 = (f32[64,30522]{1,0:T(8,128)}, f32[3,64,2048]{2,1,0:T(8,128)}, f32[3,256,512]{2,1,0:T(8,128)}) custom-call(s32[8,4,32]{2,1,0:T(4,128)} %share_ids.1.ids_ref.slot_ref, bf16[40,768,128]{2,1,0:T(8,128)(2,1)} %bitcast.16, bf16[1024,128]{1,0:T(8,128)(2,1)} %bitcast.20, f32[3,64,2048]{2,1,0:T(8,128)} %get-tuple-element.12.gin_ref, ...), custom_call_target="tpu_custom_call" | custom-call | tf_op jit(solution)/shard_map/finish/pallas_call | solution.py:572

commit v4 on v3

--- a/solution.py
+++ b/solution.py
@@ -15,7 +15,7 @@
 CHUNKS = 5
 HALF_VOCAB = VOCAB_CHUNK * CHUNKS
 WEIGHT_UNITS = 6
-FINISH_BLOCK = 3072
+FINISH_BLOCK = 6144
 UNIT_ORDER = tuple(('e', i) for i in range(CHUNKS)) + (('w', 5), ('w', 4), ('t', 0), ('w', 3), ('w', 2), ('w', 1), ('w', 0))
 GROUPS = ((0, 1), (1, 1), (2, 1), (3, 1), (4, 1))
 TOUCH_GROUP = len(GROUPS)
@@ -477,10 +477,11 @@
     pltpu.make_async_copy(emb_ref.at[pl.ds(0, replicas * tokens)], out_ref, sem).wait()
 
 
-def finish_kernel(scale, ids_ref, base_ref, patch_ref, gin_ref, gout_ref, emb_out, gin_out, gout_out, rows_f, patch_f, stage, sem):
+def finish_kernel(scale, ids_ref, base_ref, patch_ref, gin_ref, gout_ref, emb_out, gin_out, gout_out, rows_f, patch_f, stage, gin_buf, gout_buf, sem, sem_g):
     step = pl.program_id(0)
     core = lax.rem(lax.axis_index('dp'), 2)
     chunks = base_ref.shape[0]
+    moves = ((gin_ref, gin_out, gin_buf, 0), (gout_ref, gout_out, gout_buf, 1))
 
     @pl.when(step == 0)
     def _():
@@ -488,8 +489,8 @@
             return pltpu.make_async_copy(base_ref.at[i], stage.at[pl.ds(pl.multiple_of(i * VOCAB_CHUNK, VOCAB_CHUNK), VOCAB_CHUNK), :], sem.at[i])
         for i in range(chunks):
             copy(i).start()
-        gin_out[...] = gin_ref[...] * scale
-        gout_out[...] = gout_ref[...] * scale
+        for src, dst, buf, j in moves:
+            pltpu.make_async_copy(src, buf, sem_g.at[j]).start()
         patch_f[...] = patch_ref[...].astype(F32)
 
         def widen(i, carry):
@@ -501,12 +502,26 @@
 
         replicas, stages, tokens = ids_ref.shape
 
-        def put(i, carry):
-            z, r, t = i // (replicas * tokens // 8), lax.rem(i // (tokens // 8), replicas), lax.rem(i, tokens // 8) * 8
-            for j in range(8):
-                rows_f[pl.ds(ids_ref[r, stages - 1 - z, t + j], 1), :] = patch_f[pl.ds(i * 8 + j, 1), :]
-            return carry
-        lax.fori_loop(0, patch_f.shape[0] // 8, put, 0)
+        for z in range(stages):
+            def put(r, carry):
+                row = pl.multiple_of((z * replicas + r) * tokens, tokens)
+                rows = patch_f[pl.ds(row, tokens), :]
+                for t in range(tokens):
+                    rows_f[pl.ds(ids_ref[r, stages - 1 - z, t], 1), :] = rows[t:t + 1, :]
+                return carry
+            lax.fori_loop(0, replicas, put, 0)
+
+    @pl.when(step == 1)
+    def _():
+        for src, dst, buf, j in moves:
+            pltpu.make_async_copy(src, buf, sem_g.at[j]).wait()
+            buf[...] = buf[...] * scale
+            pltpu.make_async_copy(buf, dst, sem_g.at[2 + j]).start()
+
+    @pl.when(step == pl.num_programs(0) - 1)
+    def _():
+        for src, dst, buf, j in moves:
+            pltpu.make_async_copy(buf, dst, sem_g.at[2 + j]).wait()
 
     pick = lax.broadcasted_iota(jnp.int32, (64, 128), 1) == lax.broadcasted_iota(jnp.int32, (64, 128), 0) + 64 * core
     sel = jnp.where(pick, scale, 0.0).astype(BF)
@@ -573,10 +588,10 @@
             functools.partial(finish_kernel, 1.0 / replicas),
             out_shape=(jax.ShapeDtypeStruct((64, vocab), F32), jax.ShapeDtypeStruct(gin.shape, F32), jax.ShapeDtypeStruct(gout.shape, F32)),
             grid=(2 * stages * HALF_VOCAB // FINISH_BLOCK,),
-            in_specs=[smem, hbm, vm, vm, vm],
-            out_specs=(pl.BlockSpec((64, FINISH_BLOCK), lambda i: (0, i)), vm, vm),
+            in_specs=[smem, hbm, vm, hbm, hbm],
+            out_specs=(pl.BlockSpec((64, FINISH_BLOCK), lambda i: (0, i)), hbm, hbm),
             scratch_shapes=[v((2 * stages * CHUNKS * VOCAB_CHUNK, 128), F32), v((stages * replicas * tokens, 128), F32),
-                            v((2 * stages * CHUNKS * VOCAB_CHUNK, 128), BF), dma((2 * stages * CHUNKS,))],
+                            v((2 * stages * CHUNKS * VOCAB_CHUNK, 128), BF), v(gin.shape, F32), v(gout.shape, F32), dma((2 * stages * CHUNKS,)), dma((4,))],
             compiler_params=pltpu.CompilerParams(vmem_limit_bytes=58 * 2 ** 20, dimension_semantics=('arbitrary',)),
             name='finish',
         )(slot_ids, emb.reshape(2 * stages * CHUNKS, VOCAB_CHUNK, 128), patch.reshape(-1, 128), gin, gout)

time: 146 us -> 140 us (0.959)
  Pallas kernels: 143 us -> 137 us
    pallas_call x1, Pallas kernels: 17.7 us -> 12.1 us  [device_body(): pl.pallas_call(functools.partial(finish_kernel, 1.0 / replicas), out_shap...]
where the time goes in v4:
time: 140 us
  Pallas kernels  137 us (98%)
  local copies, waits for them, and re-layouts  1.44 us (1%)
    pallas_call x1, Pallas kernels, device_body(): pl.pallas_call(functools.partial(comm_kernel, stages, layers, vocab), out...  115 us
    pallas_call x1, Pallas kernels, device_body(): pl.pallas_call(functools.partial(finish_kernel, 1.0 / replicas), out_shap...  12.1 us
    pallas_call x1, Pallas kernels, device_body(): pl.pallas_call(functools.partial(share_kernel, replicas), out_shape=jax.S...  6.34 us
    pallas_call x1, Pallas kernels, device_body(): pl.pallas_call(gather_kernel, out_shape=jax.ShapeDtypeStruct((replicas *...  3.66 us

profile of v4, /device:TPU:25, one launch (start us, length us, event | category | flops | bytes accessed | tf_op | source)
XLA Modules:
  0.0 139.5 jit_solution(11790557088980961937)
XLA Ops:
  0.6 0.7 rev.3
  1.3 6.3 %share_ids.1.ids_ref.slot_ref = s32[8,4,32]{2,1,0:T(4,128)} custom-call(s32[4,32]{1,0:T(4,128)} %own_ref.1), custom_call_target="tpu_custom_call" | custom-call | tf_op jit(solution)/shard_map/share_ids/pallas_call | solution.py:548
  7.7 0.7 reshape.46.ids_ref
  8.4 3.7 %gather_rows.1 = f32[256,4,128]{2,1,0:T(4,128)} custom-call(s32[8,4,32]{2,1,0:T(4,128)} %share_ids.1.ids_ref.slot_ref, f32[30522,4,128]{2,1,0:T(4,128)} %bitcast.12), custom_call_target="tpu_custom_call" | custom-call | tf_op jit(solution)/shard_map/gather_rows/pallas_call | solution.py:556
  12.1 115.2 %reduce_exchange.1 = (f32[3,64,2048]{2,1,0:T(8,128)}, f32[3,256,512]{2,1,0:T(8,128)}, bf16[8,5,768,128]{3,2,1,0:T(8,128)(2,1)}, bf16[8,128,128]{2,1,0:T(8,128)(2,1)}) custom-call(s32[128,1]{1,0:T(8,128)} %reshape.46.ids_ref, s32[8,4,32]{2,1,0:T(4,128)} %share_ids.1.ids_ref.slot_ref, f32[1024,128]{1,0:T(8,128)} %bitcast.19, bf16[32,512]{1,0:T(8,128)(2,1)} %bitcast.22, ...), custom_call_target="tpu_custom_call" | custom-call | tf_op jit(solution)/shard_map/reduce_exchange/pallas_call | solution.py:565
  127.3 12.1 %finish.1 = (f32[64,30522]{1,0:T(8,128)}, f32[3,64,2048]{2,1,0:T(8,128)}, f32[3,256,512]{2,1,0:T(8,128)}) custom-call(s32[8,4,32]{2,1,0:T(4,128)} %share_ids.1.ids_ref.slot_ref, bf16[40,768,128]{2,1,0:T(8,128)(2,1)} %bitcast.16, bf16[1024,128]{1,0:T(8,128)(2,1)} %bitcast.20, f32[3,64,2048]{2,1,0:T(8,128)} %get-tuple-element.12.gin_ref, ...), custom_call_target="tpu_custom_call" | custom-call | tf_op jit(solution)/shard_map/finish/pallas_call | solution.py:587

commit v5 on v4

--- a/solution.py
+++ b/solution.py
@@ -15,7 +15,7 @@
 CHUNKS = 5
 HALF_VOCAB = VOCAB_CHUNK * CHUNKS
 WEIGHT_UNITS = 6
-FINISH_BLOCK = 6144
+FINISH_BLOCK = 7680
 UNIT_ORDER = tuple(('e', i) for i in range(CHUNKS)) + (('w', 5), ('w', 4), ('t', 0), ('w', 3), ('w', 2), ('w', 1), ('w', 0))
 GROUPS = ((0, 1), (1, 1), (2, 1), (3, 1), (4, 1))
 TOUCH_GROUP = len(GROUPS)
@@ -468,12 +468,11 @@
     replicas, _, tokens = ids_ref.shape
     z = ids_ref.shape[1] - 1 - lax.axis_index('pp')
 
-    def body(i, carry):
-        r, t = i // (tokens // 8), lax.rem(i, tokens // 8) * 8
-        for j in range(8):
-            pltpu.make_async_copy(emb_ref.at[ids_ref[r, z, t + j]], out_ref.at[i * 8 + j], sem).start()
+    def body(r, carry):
+        for t in range(tokens):
+            pltpu.make_async_copy(emb_ref.at[ids_ref[r, z, t]], out_ref.at[r * tokens + t], sem).start()
         return carry
-    lax.fori_loop(0, replicas * tokens // 8, body, 0)
+    lax.fori_loop(0, replicas, body, 0)
     pltpu.make_async_copy(emb_ref.at[pl.ds(0, replicas * tokens)], out_ref, sem).wait()
 
 

time: 140 us -> 140 us (level)
  no operation moved by 1% of the time
where the time goes in v5:
time: 140 us; the launch traced here: 139 us
  Pallas kernels  137 us (98%)
  local copies, waits for them, and re-layouts  1.44 us (1%)
    pallas_call x1, Pallas kernels, device_body(): pl.pallas_call(functools.partial(comm_kernel, stages, layers, vocab), out...  115 us
    pallas_call x1, Pallas kernels, device_body(): pl.pallas_call(functools.partial(finish_kernel, 1.0 / replicas), out_shap...  12 us
    pallas_call x1, Pallas kernels, device_body(): pl.pallas_call(functools.partial(share_kernel, replicas), out_shape=jax.S...  6.34 us
    pallas_call x1, Pallas kernels, device_body(): pl.pallas_call(gather_kernel, out_shape=jax.ShapeDtypeStruct((replicas *...  3.54 us

profile of v5, /device:TPU:25, one launch (start us, length us, event | category | flops | bytes accessed | tf_op | source)
XLA Modules:
  0.0 139.3 jit_solution(5093285187184909350)
XLA Ops:
  0.6 0.7 rev.3
  1.3 6.3 %share_ids.1.ids_ref.slot_ref = s32[8,4,32]{2,1,0:T(4,128)} custom-call(s32[4,32]{1,0:T(4,128)} %own_ref.1), custom_call_target="tpu_custom_call" | custom-call | tf_op jit(solution)/shard_map/share_ids/pallas_call | solution.py:547
  7.7 0.7 reshape.46.ids_ref
  8.4 3.5 %gather_rows.1 = f32[256,4,128]{2,1,0:T(4,128)} custom-call(s32[8,4,32]{2,1,0:T(4,128)} %share_ids.1.ids_ref.slot_ref, f32[30522,4,128]{2,1,0:T(4,128)} %bitcast.12), custom_call_target="tpu_custom_call" | custom-call | tf_op jit(solution)/shard_map/gather_rows/pallas_call | solution.py:555
  12.0 115.2 %reduce_exchange.1 = (f32[3,64,2048]{2,1,0:T(8,128)}, f32[3,256,512]{2,1,0:T(8,128)}, bf16[8,5,768,128]{3,2,1,0:T(8,128)(2,1)}, bf16[8,128,128]{2,1,0:T(8,128)(2,1)}) custom-call(s32[128,1]{1,0:T(8,128)} %reshape.46.ids_ref, s32[8,4,32]{2,1,0:T(4,128)} %share_ids.1.ids_ref.slot_ref, f32[1024,128]{1,0:T(8,128)} %bitcast.19, bf16[32,512]{1,0:T(8,128)(2,1)} %bitcast.22, ...), custom_call_target="tpu_custom_call" | custom-call | tf_op jit(solution)/shard_map/reduce_exchange/pallas_call | solution.py:564
  127.2 12.0 %finish.1 = (f32[64,30522]{1,0:T(8,128)}, f32[3,64,2048]{2,1,0:T(8,128)}, f32[3,256,512]{2,1,0:T(8,128)}) custom-call(s32[8,4,32]{2,1,0:T(4,128)} %share_ids.1.ids_ref.slot_ref, bf16[40,768,128]{2,1,0:T(8,128)(2,1)} %bitcast.16, bf16[1024,128]{1,0:T(8,128)(2,1)} %bitcast.20, f32[3,64,2048]{2,1,0:T(8,128)} %get-tuple-element.12.gin_ref, ...), custom_call_target="tpu_custom_call" | custom-call | tf_op jit(solution)/shard_map/finish/pallas_call | solution.py:586
